TPU v7x, 32 devices: a whole 2x2x4 slice. The times are simulated.
32 devices in a mesh: batch: 2 (over core), token: 8 (over z, x), hidden: 2 (over y).
Axes of the slice: x: 2, y: 2, z: 4, core: 2. Of those that a mesh axis runs over, the one named last changes fastest.
Arguments:
- hist_len: int32 [128], replicated, may hold values from 32 to 512, as said below
- queries: bfloat16 [32, 1536], P(None, 'token'), may hold values from -4 to 4
- history_keys: bfloat16 [384, 1536, 128], P(('batch', 'hidden'), 'token'), may hold values from -192 to 192
- cached_history_values: bfloat16 [384, 1536, 128], P(('batch', 'hidden'), 'token'), may hold values from -6 to 6
- gain_mix: float32 [1536], replicated, may hold values from 0.25 to 1.75
- w_up: bfloat16 [32, 1536, 3072], P('token', None, 'hidden'), may hold values from -0.15625 to 0.15625
- w_down: bfloat16 [32, 3072, 1536], P('token', 'hidden'), may hold values from -0.109375 to 0.109375
- gain_out: float32 [1536], replicated, may hold values from 0.25 to 1.75
Outputs:
- mixer_out: bfloat16 [128, 32, 1536], P(('batch', 'hidden'), 'token')
Inputs may be any that keep to these rules, and one draw needn't show every extreme that they name: `hist_len`: along batch+hidden, the requests of each index need between 32 and 96 slots, indices 2i and 2i + 1 need 4 * 32 slots together, and some index needs exactly 96; within an index, requests 2j and 2j + 1 need from 2 to 6 slots together.
All inputs are finite; a program needn't handle non-finite values.
Results may differ from a plain program's by a relative error of at most 0.015.
Values may be sent and summed in bfloat16 or wider, within the bound.
No kernel may reach another device: no remote copies, remote signals or barrier semaphores. Data moves between devices by JAX's collectives and lax.ppermute only.
A program may use at most 128 MiB of HBM per device.

v0:
```python
import math

import jax
import jax.numpy as jnp
from jax import lax
from jax.experimental import pallas as pl
from jax.experimental.pallas import tpu as pltpu
from jax.sharding import PartitionSpec as P


EPSILON = 1e-05
NEGATIVE_FILL = -1e30
LONGEST = 512
BLOCK_REQUESTS = 4
MIB = 1 << 20


def peer_of(index, step, count):
    if count & (count - 1) == 0:
        return index ^ step
    return (index + step) % count


def source_of(index, step, count):
    if count & (count - 1) == 0:
        return index ^ step
    return (index + count - step) % count


def exchange(value, axis, step, count):
    return lax.ppermute(value, axis, [(a, peer_of(a, step, count)) for a in range(count)])


def attention_kernel(sizes, len_hbm, query_hbm, key_hbm, value_hbm, *rest):
    tokens, heads, requests, head_size, positions, slots = sizes
    send, len_ref, query_ref, key_buf, value_buf, query_f32, query_diag, first_ref, sems, small = rest
    width = heads * head_size
    lane_tiles = send.shape[0]
    blocks = requests // BLOCK_REQUESTS
    chunk = slots // blocks
    depth = -(-LONGEST // positions)

    def copies(block):
        where = pl.ds(block * chunk, chunk)
        return (
            pltpu.make_async_copy(key_hbm.at[where], key_buf.at[where], sems.at[0, block]),
            pltpu.make_async_copy(value_hbm.at[where], value_buf.at[where], sems.at[1, block]),
        )

    len_copy = pltpu.make_async_copy(len_hbm, len_ref, small.at[0])
    query_copy = pltpu.make_async_copy(query_hbm, query_ref, small.at[1])
    len_copy.start()
    query_copy.start()
    for block in range(blocks):
        for copy in copies(block):
            copy.start()
    len_copy.wait()

    group = lax.axis_index(("batch", "hidden"))
    base = group * requests

    def place(r, first):
        first_ref[r] = first
        return first + (len_ref[base + r] + (positions - 1)) // positions

    lax.fori_loop(0, requests, place, jnp.int32(0))

    query_copy.wait()
    query_f32[...] = query_ref[...].astype(jnp.float32)
    column_head = lax.broadcasted_iota(jnp.int32, (tokens, width), 1) // head_size
    for i in range(heads):
        rows = jnp.concatenate(
            [query_f32[d * heads + i : d * heads + i + 1, :] for d in range(tokens)], axis=0
        )
        for h in range(heads):
            start = (i * heads + h) * tokens
            query_diag[start : start + tokens, :] = jnp.where(column_head == h, rows, 0.0)
    queries = query_diag[...].astype(jnp.bfloat16)
    factor = math.log2(math.e) * head_size ** (-0.5)
    lane = lax.broadcasted_iota(jnp.int32, (1, depth * positions), 1)

    def block_body(block, carry):
        for copy in copies(block):
            copy.wait()
        last = (block + 1) * chunk - 1
        for offset in range(BLOCK_REQUESTS):
            r = block * BLOCK_REQUESTS + offset
            first = first_ref[r]
            length = len_ref[base + r]
            index = [jnp.minimum(first + b, last) for b in range(depth)]
            keys = jnp.concatenate([key_buf[n] for n in index], axis=1)
            values = jnp.concatenate([value_buf[n] for n in index], axis=1)
            scores = jnp.dot(queries, keys, preferred_element_type=jnp.float32)
            scores = jnp.where(lane < length, scores, NEGATIVE_FILL)
            top = jnp.max(scores, axis=1, keepdims=True)
            terms = jnp.exp2((scores - top) * factor)
            total = jnp.sum(terms, axis=1, keepdims=True)
            acc = lax.dot_general(
                terms.astype(jnp.bfloat16),
                values,
                (((1,), (1,)), ((), ())),
                preferred_element_type=jnp.float32,
            )
            acc = acc / total
            for i in range(heads):
                start = i * heads * tokens
                kept = acc[start : start + tokens]
                for h in range(1, heads):
                    begin = start + h * tokens
                    kept = jnp.where(column_head >= h, acc[begin : begin + tokens], kept)
                spare = lane_tiles * 128 - width
                if spare:
                    kept = jnp.concatenate([kept, jnp.zeros((tokens, spare), jnp.float32)], axis=1)
                for tile in range(lane_tiles):
                    send[tile, pl.ds(i * requests + r, tokens, stride=heads * requests), :] = kept[
                        :, tile * 128 : (tile + 1) * 128
                    ]
        return carry

    lax.fori_loop(0, blocks, block_body, jnp.int32(0))


def pack_kernel(sizes, send, *outs):
    tokens, rows, width = sizes
    lane_tiles = send.shape[0]
    mine = lax.axis_index("token")
    for out, step in zip(outs, message_order(tokens)):
        d = peer_of(mine, step, tokens)
        where = pl.ds(pl.multiple_of(d * rows, rows), rows)
        values = jnp.concatenate([send[tile, where, :] for tile in range(lane_tiles)], axis=1)
        out[...] = values[:, :width].astype(jnp.bfloat16)


def message_order(tokens):
    return [0] + list(range(tokens - 1, 0, -1))


def pack(send, tokens, requests, heads, width):
    rows = heads * requests
    outs = pl.pallas_call(
        lambda *refs: pack_kernel((tokens, rows, width), *refs),
        out_shape=[jax.ShapeDtypeStruct((rows, width), jnp.bfloat16)] * tokens,
        in_specs=[pl.BlockSpec(memory_space=pltpu.VMEM)],
        out_specs=[pl.BlockSpec(memory_space=pltpu.VMEM)] * tokens,
        compiler_params=pltpu.CompilerParams(vmem_limit_bytes=4 * MIB),
        cost_estimate=pl.CostEstimate(
            flops=30_000_000_000, transcendentals=0, bytes_accessed=200_000_000
        ),
        name="pack",
    )(send)
    return dict(zip(message_order(tokens), outs))


def attention(hist_len, queries, keys, values, tokens, requests):
    slots, width, positions = keys.shape
    heads = queries.shape[0] // tokens
    head_size = width // heads
    blocks = requests // BLOCK_REQUESTS
    lane_tiles = -(-width // 128)
    flops = 4 * requests * LONGEST * heads * heads * tokens * width
    return pl.pallas_call(
        lambda *refs: attention_kernel((tokens, heads, requests, head_size, positions, slots), *refs),
        out_shape=jax.ShapeDtypeStruct((lane_tiles, tokens * heads * requests, 128), jnp.float32),
        in_specs=[pl.BlockSpec(memory_space=pltpu.MemorySpace.HBM)] * 4,
        out_specs=pl.BlockSpec(memory_space=pltpu.VMEM),
        scratch_shapes=[
            pltpu.SMEM(hist_len.shape, jnp.int32),
            pltpu.VMEM(queries.shape, queries.dtype),
            pltpu.VMEM(keys.shape, keys.dtype),
            pltpu.VMEM(values.shape, values.dtype),
            pltpu.VMEM(queries.shape, jnp.float32),
            pltpu.VMEM((heads * heads * tokens, width), jnp.float32),
            pltpu.SMEM((requests,), jnp.int32),
            pltpu.SemaphoreType.DMA((2, blocks)),
            pltpu.SemaphoreType.DMA((2,)),
        ],
        compiler_params=pltpu.CompilerParams(vmem_limit_bytes=16 * MIB),
        cost_estimate=pl.CostEstimate(
            flops=flops, transcendentals=flops // 400, bytes_accessed=2 * keys.size * 2
        ),
        name="attention",
    )(*[pltpu.with_memory_space_constraint(x, pltpu.HBM) for x in (hist_len, queries, keys, values)])


def norm_rows(rows):
    average = jnp.mean(rows, axis=-1, keepdims=True)
    centred = rows - average
    variance = jnp.mean(centred * centred, axis=-1, keepdims=True)
    return centred * lax.rsqrt(variance + EPSILON)


def mix_kernel(sizes, *refs):
    tokens, heads, requests, head_size, j = sizes
    sent = refs[:tokens]
    received = refs[tokens : 2 * tokens]
    gain_ref, out_ref, joined = refs[2 * tokens :]
    mine = lax.axis_index("token")
    for step in range(tokens):
        s = source_of(mine, step, tokens)
        own = sent[peer_step(step, tokens)]
        mixed = jnp.concatenate(
            [
                own[h * requests : (h + 1) * requests, j * head_size : (j + 1) * head_size]
                for h in range(heads)
            ],
            axis=1,
        )
        unmixed = received[step][j * requests : (j + 1) * requests, :]
        joined[s] = mixed.astype(jnp.float32) + unmixed.astype(jnp.float32)
    rows = jnp.concatenate([joined[s] for s in range(tokens)], axis=1)
    out_ref[...] = (norm_rows(rows) * gain_ref[...]).astype(jnp.bfloat16)


def peer_step(step, count):
    if count & (count - 1) == 0:
        return step
    return (count - step) % count


def mix(sent, received, gain, j, tokens, requests):
    heads = sent[0].shape[0] // requests
    width = sent[0].shape[1]
    model = gain.shape[1]
    return pl.pallas_call(
        lambda *refs: mix_kernel((tokens, heads, requests, width // heads, j), *refs),
        out_shape=jax.ShapeDtypeStruct((requests, model), jnp.bfloat16),
        scratch_shapes=[pltpu.VMEM((tokens, requests, width), jnp.float32)],
        compiler_params=pltpu.CompilerParams(vmem_limit_bytes=8 * MIB),
        cost_estimate=pl.CostEstimate(
            flops=10 * requests * model, transcendentals=0, bytes_accessed=6 * requests * model
        ),
        name="mix",
    )(*sent, *received, gain)


def ffn_kernel(sizes, *refs):
    j, peers = sizes
    rows = refs[:peers]
    up_ref, down_ref = refs[peers : peers + 2]
    outs = refs[peers + 2 :]
    x = jnp.concatenate([ref[...] for ref in rows], axis=0)
    lifted = jnp.dot(x, up_ref[j], preferred_element_type=jnp.float32)
    activated = (0.5 * lifted * (1.0 + lax.erf(lifted * math.sqrt(0.5)))).astype(jnp.bfloat16)
    total = jnp.dot(activated, down_ref[j], preferred_element_type=jnp.float32)
    count = rows[0].shape[0]
    for k in range(peers):
        outs[k][...] = total[k * count : (k + 1) * count].astype(outs[k].dtype)


def ffn(rows, w_up, w_down, j):
    _, model, hidden = w_up.shape
    peers = len(rows)
    count = rows[0].shape[0]
    return pl.pallas_call(
        lambda *refs: ffn_kernel((j, peers), *refs),
        out_shape=[
            jax.ShapeDtypeStruct((count, model), jnp.float32 if k == 0 else jnp.bfloat16)
            for k in range(peers)
        ],
        in_specs=[pl.BlockSpec(memory_space=pltpu.VMEM)] * (peers + 2),
        out_specs=[pl.BlockSpec(memory_space=pltpu.VMEM)] * peers,
        compiler_params=pltpu.CompilerParams(vmem_limit_bytes=8 * MIB),
        cost_estimate=pl.CostEstimate(
            flops=4 * peers * count * model * hidden,
            transcendentals=peers * count * hidden,
            bytes_accessed=4 * model * hidden,
        ),
        name="ffn",
    )(*rows, w_up, w_down)


def finish_kernel(sizes, *refs):
    heads, parts = sizes
    gain_ref, out_ref = refs[heads * parts :]
    for j in range(heads):
        summed = refs[j * parts][...]
        for ref in refs[j * parts + 1 : (j + 1) * parts]:
            summed = summed + ref[...].astype(jnp.float32)
        out_ref[:, j, :] = (norm_rows(summed) * gain_ref[...]).astype(jnp.bfloat16)


def finish(terms, gain):
    heads, parts = len(terms), len(terms[0])
    count, model = terms[0][0].shape
    return pl.pallas_call(
        lambda *refs: finish_kernel((heads, parts), *refs),
        out_shape=jax.ShapeDtypeStruct((count, heads, model), jnp.bfloat16),
        compiler_params=pltpu.CompilerParams(vmem_limit_bytes=16 * MIB),
        cost_estimate=pl.CostEstimate(
            flops=10 * heads * count * model, transcendentals=0, bytes_accessed=8 * heads * count * model
        ),
        name="finish",
    )(*[part for token in terms for part in token], gain)


def local(hist_len, queries, history_keys, cached_history_values, gain_mix, w_up, w_down, gain_out):
    tokens = lax.axis_size("token")
    sides = lax.axis_size("hidden")
    groups = lax.axis_size("batch") * sides
    requests = hist_len.shape[0] // groups
    heads = queries.shape[0] // tokens
    w_up = pltpu.with_memory_space_constraint(w_up, pltpu.VMEM)
    w_down = pltpu.with_memory_space_constraint(w_down, pltpu.VMEM)
    send = attention(hist_len, queries, history_keys, cached_history_values, tokens, requests)
    messages = pack(send, tokens, requests, heads, history_keys.shape[1])
    arrived = {0: messages[0]}
    for k in message_order(tokens)[1:]:
        arrived[k] = exchange(messages[k], "token", k, tokens)
    sent = [messages[k] for k in range(tokens)]
    received = [arrived[k] for k in range(tokens)]
    gain_mix = gain_mix.reshape(1, -1)
    gain_out = gain_out.reshape(1, -1)
    normed = [mix(sent, received, gain_mix, j, tokens, requests) for j in range(heads)]
    terms = []
    for j in range(heads):
        rows = [normed[j]] + [exchange(normed[j], "hidden", k, sides) for k in range(1, sides)]
        parts = ffn(rows, w_up, w_down, j)
        back = [
            exchange(parts[k], "hidden", peer_step(k, sides), sides) for k in range(1, sides)
        ]
        terms.append([parts[0]] + back + [normed[j]])
    return finish(terms, gain_out)


def solution(mesh):
    return jax.shard_map(
        local,
        mesh=mesh,
        in_specs=(
            P(),
            P(None, "token"),
            P(("batch", "hidden"), "token", None),
            P(("batch", "hidden"), "token", None),
            P(),
            P("token", None, "hidden"),
            P("token", "hidden", None),
            P(),
        ),
        out_specs=P(("batch", "hidden"), "token", None),
        check_vma=False,
    )
```

profile of v0, /device:TPU:0, one launch (start us, length us, event | category | flops | bytes accessed | tf_op | source)
XLA Modules:
  0.0 53.8 jit_solution(1835082842242867166)
XLA Ops:
  0.0 11.1 %attention.1.refs_0_ = f32[2,1024,128]{2,1,0:T(8,128)S(1)} custom-call(s32[128]{0:T(128)} %refs_0_.1, bf16[32,192]{1,0:T(8,128)(2,1)} %refs_1_.1, bf16[96,192,128]{2,1,0:T(8,128)(2,1)} %refs_2_.5, bf16[96,192,128]{2,1,0:T(8,128)(2,1)} %refs_3_.5), custom_call_target="tpu_custom_call" | custom-call | flops 1610612736 | bytes 9437184 | tf_op jit(solution)/shard_map/attention/pallas_call | solution.py:161
  11.1 0.0 copy-start
  11.1 0.0 slice-start.1
  11.1 0.0 slice-start.6
  11.2 0.1 pack.1
  11.3 3.0 %collective-permute-start = (bf16[128,192]{1,0:T(8,128)(2,1)S(1)}, bf16[128,192]{1,0:T(8,128)(2,1)S(1)}, u32[]{:S(2)}, u32[]{:S(2)}) collective-permute-start(bf16[128,192]{1,0:T(8,128)(2,1)S(1)} %get-tuple-element.22.refs_1_), channel_id=1, source_target_pairs={{0,2},{2,0},{4,6},{6,4},{8,10},{10,8},{12,14},{14,12},{1,3},{3,1},... | collective-permute-start | bytes 147464 | tf_op jit(solution)/shard_map/ppermute | solution.py:31
  14.3 1.6 %collective-permute-start.1 = (bf16[128,192]{1,0:T(8,128)(2,1)S(1)}, bf16[128,192]{1,0:T(8,128)(2,1)S(1)}, u32[]{:S(2)}, u32[]{:S(2)}) collective-permute-start(bf16[128,192]{1,0:T(8,128)(2,1)S(1)} %get-tuple-element.23.refs_2_), channel_id=1, source_target_pairs={{0,4},{2,6},{4,0},{6,2},{8,12},{10,14},{12,8},{14,10},{1,5},{3,7},... | collective-permute-start | bytes 147464 | tf_op jit(solution)/shard_map/ppermute | solution.py:31
  15.9 3.0 %collective-permute-start.3 = (bf16[128,192]{1,0:T(8,128)(2,1)S(1)}, bf16[128,192]{1,0:T(8,128)(2,1)S(1)}, u32[]{:S(2)}, u32[]{:S(2)}) collective-permute-start(bf16[128,192]{1,0:T(8,128)(2,1)S(1)} %get-tuple-element.25.refs_4_), channel_id=1, source_target_pairs={{0,8},{2,10},{4,12},{6,14},{8,0},{10,2},{12,4},{14,6},{1,9},{3,11}... | collective-permute-start | bytes 147464 | tf_op jit(solution)/shard_map/ppermute | solution.py:31
  18.9 1.3 %collective-permute-start.4 = (bf16[128,192]{1,0:T(8,128)(2,1)S(1)}, bf16[128,192]{1,0:T(8,128)(2,1)S(1)}, u32[]{:S(2)}, u32[]{:S(2)}) collective-permute-start(bf16[128,192]{1,0:T(8,128)(2,1)S(1)} %get-tuple-element.26.refs_5_), channel_id=1, source_target_pairs={{0,10},{2,8},{4,14},{6,12},{8,2},{10,0},{12,6},{14,4},{1,11},{3,9}... | collective-permute-start | bytes 147464 | tf_op jit(solution)/shard_map/ppermute | solution.py:31
  20.1 3.6 %collective-permute-start.5 = (bf16[128,192]{1,0:T(8,128)(2,1)S(1)}, bf16[128,192]{1,0:T(8,128)(2,1)S(1)}, u32[]{:S(2)}, u32[]{:S(2)}) collective-permute-start(bf16[128,192]{1,0:T(8,128)(2,1)S(1)} %get-tuple-element.27.refs_6_), channel_id=1, source_target_pairs={{0,12},{2,14},{4,8},{6,10},{8,4},{10,6},{12,0},{14,2},{1,13},{3,15... | collective-permute-start | bytes 147464 | tf_op jit(solution)/shard_map/ppermute | solution.py:31
  23.8 0.0 collective-permute-start.6
  23.8 5.2 %collective-permute-done.4.refs_13_ = bf16[128,192]{1,0:T(8,128)(2,1)S(1)} collective-permute-done((bf16[128,192]{1,0:T(8,128)(2,1)S(1)}, bf16[128,192]{1,0:T(8,128)(2,1)S(1)}, u32[]{:S(2)}, u32[]{:S(2)}) %collective-permute-start.4) | collective-permute-done | bytes 49184 | tf_op jit(solution)/shard_map/ppermute | solution.py:31
  29.1 1.8 %collective-permute-done.6.refs_15_ = bf16[128,192]{1,0:T(8,128)(2,1)S(1)} collective-permute-done((bf16[128,192]{1,0:T(8,128)(2,1)S(1)}, bf16[128,192]{1,0:T(8,128)(2,1)S(1)}, u32[]{:S(2)}, u32[]{:S(2)}) %collective-permute-start.6) | collective-permute-done | bytes 49184 | tf_op jit(solution)/shard_map/ppermute | solution.py:31
  30.8 0.4 mix.7.refs_0_.refs_11_
  31.3 1.6 %collective-permute-start.13 = (bf16[32,1536]{1,0:T(8,128)(2,1)S(1)}, bf16[32,1536]{1,0:T(8,128)(2,1)S(1)}, u32[]{:S(2)}, u32[]{:S(2)}) collective-permute-start(bf16[32,1536]{1,0:T(8,128)(2,1)S(1)} %mix.7.refs_0_.refs_11_), channel_id=1, source_target_pairs={{0,1},{1,0},{2,3},{3,2},{4,5},{5,4},{6,7},{7,6},{8,9},{9,8},{10,11... | collective-permute-start | bytes 294920 | tf_op jit(solution)/shard_map/ppermute | solution.py:31
  32.8 0.5 mix.6.refs_0_.refs_8_
  33.3 0.6 %collective-permute-start.11 = (bf16[32,1536]{1,0:T(8,128)(2,1)S(1)}, bf16[32,1536]{1,0:T(8,128)(2,1)S(1)}, u32[]{:S(2)}, u32[]{:S(2)}) collective-permute-start(bf16[32,1536]{1,0:T(8,128)(2,1)S(1)} %mix.6.refs_0_.refs_8_), channel_id=1, source_target_pairs={{0,1},{1,0},{2,3},{3,2},{4,5},{5,4},{6,7},{7,6},{8,9},{9,8},{10,11... | collective-permute-start | bytes 294920 | tf_op jit(solution)/shard_map/ppermute | solution.py:31
  33.9 0.4 mix.4.refs_0_.refs_2_
  34.3 1.6 %collective-permute-start.7 = (bf16[32,1536]{1,0:T(8,128)(2,1)S(1)}, bf16[32,1536]{1,0:T(8,128)(2,1)S(1)}, u32[]{:S(2)}, u32[]{:S(2)}) collective-permute-start(bf16[32,1536]{1,0:T(8,128)(2,1)S(1)} %mix.4.refs_0_.refs_2_), channel_id=1, source_target_pairs={{0,1},{1,0},{2,3},{3,2},{4,5},{5,4},{6,7},{7,6},{8,9},{9,8},{10,11... | collective-permute-start | bytes 294920 | tf_op jit(solution)/shard_map/ppermute | solution.py:31
  35.9 0.4 mix.5.refs_0_.refs_5_
  36.3 0.6 %collective-permute-start.9 = (bf16[32,1536]{1,0:T(8,128)(2,1)S(1)}, bf16[32,1536]{1,0:T(8,128)(2,1)S(1)}, u32[]{:S(2)}, u32[]{:S(2)}) collective-permute-start(bf16[32,1536]{1,0:T(8,128)(2,1)S(1)} %mix.5.refs_0_.refs_5_), channel_id=1, source_target_pairs={{0,1},{1,0},{2,3},{3,2},{4,5},{5,4},{6,7},{7,6},{8,9},{9,8},{10,11... | collective-permute-start | bytes 294920 | tf_op jit(solution)/shard_map/ppermute | solution.py:31
  37.0 1.8 %ffn.7 = (f32[32,1536]{1,0:T(8,128)S(1)}, bf16[32,1536]{1,0:T(8,128)(2,1)S(1)}) custom-call(bf16[32,1536]{1,0:T(8,128)(2,1)S(1)} %mix.7.refs_0_.refs_11_, bf16[32,1536]{1,0:T(8,128)(2,1)S(1)} %collective-permute-done.13.refs_1_, bf16[4,1536,1536]{2,1,0:T(8,128)(2,1)S(1)} %bitcast.1, bf16[4,1536,1536]{2,1,0:T(8,128)(2,1)S(1)} %bitcast.3), custom_call_target="tpu_custom_call" | custom-call | flops 603979776 | bytes 9437184 | tf_op jit(solution)/shard_map/ffn/pallas_call | solution.py:254
  38.8 1.6 %collective-permute-start.14 = (bf16[32,1536]{1,0:T(8,128)(2,1)S(1)}, bf16[32,1536]{1,0:T(8,128)(2,1)S(1)}, u32[]{:S(2)}, u32[]{:S(2)}) collective-permute-start(bf16[32,1536]{1,0:T(8,128)(2,1)S(1)} %get-tuple-element.36), channel_id=1, source_target_pairs={{0,1},{1,0},{2,3},{3,2},{4,5},{5,4},{6,7},{7,6},{8,9},{9,8},{10,11... | collective-permute-start | bytes 294920 | tf_op jit(solution)/shard_map/ppermute | solution.py:31
  40.3 1.8 %ffn.6 = (f32[32,1536]{1,0:T(8,128)S(1)}, bf16[32,1536]{1,0:T(8,128)(2,1)S(1)}) custom-call(bf16[32,1536]{1,0:T(8,128)(2,1)S(1)} %mix.6.refs_0_.refs_8_, bf16[32,1536]{1,0:T(8,128)(2,1)S(1)} %collective-permute-done.11.refs_1_, bf16[4,1536,1536]{2,1,0:T(8,128)(2,1)S(1)} %bitcast.1, bf16[4,1536,1536]{2,1,0:T(8,128)(2,1)S(1)} %bitcast.3), custom_call_target="tpu_custom_call" | custom-call | flops 603979776 | bytes 9437184 | tf_op jit(solution)/shard_map/ffn/pallas_call | solution.py:254
  42.1 0.6 %collective-permute-start.12 = (bf16[32,1536]{1,0:T(8,128)(2,1)S(1)}, bf16[32,1536]{1,0:T(8,128)(2,1)S(1)}, u32[]{:S(2)}, u32[]{:S(2)}) collective-permute-start(bf16[32,1536]{1,0:T(8,128)(2,1)S(1)} %get-tuple-element.34), channel_id=1, source_target_pairs={{0,1},{1,0},{2,3},{3,2},{4,5},{5,4},{6,7},{7,6},{8,9},{9,8},{10,11... | collective-permute-start | bytes 294920 | tf_op jit(solution)/shard_map/ppermute | solution.py:31
  42.7 1.8 %ffn.5 = (f32[32,1536]{1,0:T(8,128)S(1)}, bf16[32,1536]{1,0:T(8,128)(2,1)S(1)}) custom-call(bf16[32,1536]{1,0:T(8,128)(2,1)S(1)} %mix.5.refs_0_.refs_5_, bf16[32,1536]{1,0:T(8,128)(2,1)S(1)} %collective-permute-done.9.refs_1_, bf16[4,1536,1536]{2,1,0:T(8,128)(2,1)S(1)} %bitcast.1, bf16[4,1536,1536]{2,1,0:T(8,128)(2,1)S(1)} %bitcast.3), custom_call_target="tpu_custom_call" | custom-call | flops 603979776 | bytes 9437184 | tf_op jit(solution)/shard_map/ffn/pallas_call | solution.py:254
  44.5 1.6 %collective-permute-start.10 = (bf16[32,1536]{1,0:T(8,128)(2,1)S(1)}, bf16[32,1536]{1,0:T(8,128)(2,1)S(1)}, u32[]{:S(2)}, u32[]{:S(2)}) collective-permute-start(bf16[32,1536]{1,0:T(8,128)(2,1)S(1)} %get-tuple-element.32), channel_id=1, source_target_pairs={{0,1},{1,0},{2,3},{3,2},{4,5},{5,4},{6,7},{7,6},{8,9},{9,8},{10,11... | collective-permute-start | bytes 294920 | tf_op jit(solution)/shard_map/ppermute | solution.py:31
  46.0 1.8 %ffn.4 = (f32[32,1536]{1,0:T(8,128)S(1)}, bf16[32,1536]{1,0:T(8,128)(2,1)S(1)}) custom-call(bf16[32,1536]{1,0:T(8,128)(2,1)S(1)} %mix.4.refs_0_.refs_2_, bf16[32,1536]{1,0:T(8,128)(2,1)S(1)} %collective-permute-done.7.refs_1_, bf16[4,1536,1536]{2,1,0:T(8,128)(2,1)S(1)} %bitcast.1, bf16[4,1536,1536]{2,1,0:T(8,128)(2,1)S(1)} %bitcast.3), custom_call_target="tpu_custom_call" | custom-call | flops 603979776 | bytes 9437184 | tf_op jit(solution)/shard_map/ffn/pallas_call | solution.py:254
  47.8 0.6 %collective-permute-start.8 = (bf16[32,1536]{1,0:T(8,128)(2,1)S(1)}, bf16[32,1536]{1,0:T(8,128)(2,1)S(1)}, u32[]{:S(2)}, u32[]{:S(2)}) collective-permute-start(bf16[32,1536]{1,0:T(8,128)(2,1)S(1)} %get-tuple-element.30), channel_id=1, source_target_pairs={{0,1},{1,0},{2,3},{3,2},{4,5},{5,4},{6,7},{7,6},{8,9},{9,8},{10,11... | collective-permute-start | bytes 294920 | tf_op jit(solution)/shard_map/ppermute | solution.py:31
  48.4 0.7 %collective-permute-done.10.refs_4_ = bf16[32,1536]{1,0:T(8,128)(2,1)S(1)} collective-permute-done((bf16[32,1536]{1,0:T(8,128)(2,1)S(1)}, bf16[32,1536]{1,0:T(8,128)(2,1)S(1)}, u32[]{:S(2)}, u32[]{:S(2)}) %collective-permute-start.10) | collective-permute-done | bytes 98336 | tf_op jit(solution)/shard_map/ppermute | solution.py:31
  49.1 3.3 %collective-permute-done.8.refs_1_ = bf16[32,1536]{1,0:T(8,128)(2,1)S(1)} collective-permute-done((bf16[32,1536]{1,0:T(8,128)(2,1)S(1)}, bf16[32,1536]{1,0:T(8,128)(2,1)S(1)}, u32[]{:S(2)}, u32[]{:S(2)}) %collective-permute-start.8) | collective-permute-done | bytes 98336 | tf_op jit(solution)/shard_map/ppermute | solution.py:31
  52.5 1.3 %finish.1 = bf16[32,4,1536]{2,1,0:T(4,128)(2,1)} custom-call(f32[32,1536]{1,0:T(8,128)S(1)} %get-tuple-element.29.refs_0_, bf16[32,1536]{1,0:T(8,128)(2,1)S(1)} %collective-permute-done.8.refs_1_, bf16[32,1536]{1,0:T(8,128)(2,1)S(1)} %mix.4.refs_0_.refs_2_, f32[32,1536]{1,0:T(8,128)S(1)} %get-tuple-element.31.refs_3_, ...), custom_call_target="tpu_custom_call" | custom-call | flops 1966080 | bytes 1572864 | tf_op jit(solution)/shard_map/finish/pallas_call | solution.py:285
  (37 shorter events, 0.1 us)
Async XLA Ops:
  0.0 36.9 %slice-start = ((s8[18874368]{0:T(1024)(128)(4,1)}), s8[4194304]{0:T(1024)(128)(4,1)S(1)}, s32[]{:S(2)}) async-start(s8[18874368]{0:T(1024)(128)(4,1)} %bitcast), calls=%async_computation | async-start | bytes 8388608
  0.0 36.9 %slice-start.5 = ((s8[18874368]{0:T(1024)(128)(4,1)}), s8[2097152]{0:T(1024)(128)(4,1)S(1)}, s32[]{:S(2)}) async-start(s8[18874368]{0:T(1024)(128)(4,1)} %bitcast.2), calls=%async_computation.5 | async-start | bytes 4194304
  11.1 12.7 %copy-start = (f32[1536]{0:T(1024)S(1)}, f32[1536]{0:T(1024)}, u32[]{:S(2)}) copy-start(f32[1536]{0:T(1024)} %param.12) | copy-start | bytes 18436
  11.1 25.8 %slice-start.1 = ((s8[18874368]{0:T(1024)(128)(4,1)}), s8[4194304]{0:T(1024)(128)(4,1)S(1)}, s32[]{:S(2)}) async-start(s8[18874368]{0:T(1024)(128)(4,1)} %bitcast), calls=%async_computation.1 | async-start | bytes 8388608
  11.1 25.8 %slice-start.2 = ((s8[18874368]{0:T(1024)(128)(4,1)}), s8[4194304]{0:T(1024)(128)(4,1)S(1)}, s32[]{:S(2)}) async-start(s8[18874368]{0:T(1024)(128)(4,1)} %bitcast), calls=%async_computation.2 | async-start | bytes 8388608
  11.1 25.8 %slice-start.3 = ((s8[18874368]{0:T(1024)(128)(4,1)}), s8[4194304]{0:T(1024)(128)(4,1)S(1)}, s32[]{:S(2)}) async-start(s8[18874368]{0:T(1024)(128)(4,1)} %bitcast), calls=%async_computation.3 | async-start | bytes 8388608
  11.1 25.8 %slice-start.4 = ((s8[18874368]{0:T(1024)(128)(4,1)}), s8[2097152]{0:T(1024)(128)(4,1)S(1)}, s32[]{:S(2)}) async-start(s8[18874368]{0:T(1024)(128)(4,1)} %bitcast), calls=%async_computation.4 | async-start | bytes 4194304
  11.1 25.8 %slice-start.6 = ((s8[18874368]{0:T(1024)(128)(4,1)}), s8[4194304]{0:T(1024)(128)(4,1)S(1)}, s32[]{:S(2)}) async-start(s8[18874368]{0:T(1024)(128)(4,1)} %bitcast.2), calls=%async_computation.6 | async-start | bytes 8388608
  11.2 25.8 %slice-start.7 = ((s8[18874368]{0:T(1024)(128)(4,1)}), s8[4194304]{0:T(1024)(128)(4,1)S(1)}, s32[]{:S(2)}) async-start(s8[18874368]{0:T(1024)(128)(4,1)} %bitcast.2), calls=%async_computation.7 | async-start | bytes 8388608
  11.2 25.8 %slice-start.8 = ((s8[18874368]{0:T(1024)(128)(4,1)}), s8[4194304]{0:T(1024)(128)(4,1)S(1)}, s32[]{:S(2)}) async-start(s8[18874368]{0:T(1024)(128)(4,1)} %bitcast.2), calls=%async_computation.8 | async-start | bytes 8388608
  11.2 25.8 %slice-start.9 = ((s8[18874368]{0:T(1024)(128)(4,1)}), s8[4194304]{0:T(1024)(128)(4,1)S(1)}, s32[]{:S(2)}) async-start(s8[18874368]{0:T(1024)(128)(4,1)} %bitcast.2), calls=%async_computation.9 | async-start | bytes 8388608
  11.3 8.9 %collective-permute-start = (bf16[128,192]{1,0:T(8,128)(2,1)S(1)}, bf16[128,192]{1,0:T(8,128)(2,1)S(1)}, u32[]{:S(2)}, u32[]{:S(2)}) collective-permute-start(bf16[128,192]{1,0:T(8,128)(2,1)S(1)} %get-tuple-element.22.refs_1_), channel_id=1, source_target_pairs={{0,2},{2,0},{4,6},{6,4},{8,10},{10,8},{12,14},{14,12},{1,3},{3,1},... | collective-permute-start | bytes 147464 | tf_op jit(solution)/shard_map/ppermute | solution.py:31
  14.3 9.5 %collective-permute-start.1 = (bf16[128,192]{1,0:T(8,128)(2,1)S(1)}, bf16[128,192]{1,0:T(8,128)(2,1)S(1)}, u32[]{:S(2)}, u32[]{:S(2)}) collective-permute-start(bf16[128,192]{1,0:T(8,128)(2,1)S(1)} %get-tuple-element.23.refs_2_), channel_id=1, source_target_pairs={{0,4},{2,6},{4,0},{6,2},{8,12},{10,14},{12,8},{14,10},{1,5},{3,7},... | collective-permute-start | bytes 147464 | tf_op jit(solution)/shard_map/ppermute | solution.py:31
  15.9 7.9 %collective-permute-start.2 = (bf16[128,192]{1,0:T(8,128)(2,1)S(1)}, bf16[128,192]{1,0:T(8,128)(2,1)S(1)}, u32[]{:S(2)}, u32[]{:S(2)}) collective-permute-start(bf16[128,192]{1,0:T(8,128)(2,1)S(1)} %get-tuple-element.24.refs_3_), channel_id=1, source_target_pairs={{0,6},{2,4},{4,2},{6,0},{8,14},{10,12},{12,10},{14,8},{1,7},{3,5},... | collective-permute-start | bytes 147464 | tf_op jit(solution)/shard_map/ppermute | solution.py:31
  15.9 7.9 %collective-permute-start.3 = (bf16[128,192]{1,0:T(8,128)(2,1)S(1)}, bf16[128,192]{1,0:T(8,128)(2,1)S(1)}, u32[]{:S(2)}, u32[]{:S(2)}) collective-permute-start(bf16[128,192]{1,0:T(8,128)(2,1)S(1)} %get-tuple-element.25.refs_4_), channel_id=1, source_target_pairs={{0,8},{2,10},{4,12},{6,14},{8,0},{10,2},{12,4},{14,6},{1,9},{3,11}... | collective-permute-start | bytes 147464 | tf_op jit(solution)/shard_map/ppermute | solution.py:31
  18.9 10.2 %collective-permute-start.4 = (bf16[128,192]{1,0:T(8,128)(2,1)S(1)}, bf16[128,192]{1,0:T(8,128)(2,1)S(1)}, u32[]{:S(2)}, u32[]{:S(2)}) collective-permute-start(bf16[128,192]{1,0:T(8,128)(2,1)S(1)} %get-tuple-element.26.refs_5_), channel_id=1, source_target_pairs={{0,10},{2,8},{4,14},{6,12},{8,2},{10,0},{12,6},{14,4},{1,11},{3,9}... | collective-permute-start | bytes 147464 | tf_op jit(solution)/shard_map/ppermute | solution.py:31
  20.1 8.9 %collective-permute-start.5 = (bf16[128,192]{1,0:T(8,128)(2,1)S(1)}, bf16[128,192]{1,0:T(8,128)(2,1)S(1)}, u32[]{:S(2)}, u32[]{:S(2)}) collective-permute-start(bf16[128,192]{1,0:T(8,128)(2,1)S(1)} %get-tuple-element.27.refs_6_), channel_id=1, source_target_pairs={{0,12},{2,14},{4,8},{6,10},{8,4},{10,6},{12,0},{14,2},{1,13},{3,15... | collective-permute-start | bytes 147464 | tf_op jit(solution)/shard_map/ppermute | solution.py:31
  23.8 7.1 %collective-permute-start.6 = (bf16[128,192]{1,0:T(8,128)(2,1)S(1)}, bf16[128,192]{1,0:T(8,128)(2,1)S(1)}, u32[]{:S(2)}, u32[]{:S(2)}) collective-permute-start(bf16[128,192]{1,0:T(8,128)(2,1)S(1)} %get-tuple-element.28.refs_7_), channel_id=1, source_target_pairs={{0,14},{2,12},{4,10},{6,8},{8,6},{10,4},{12,2},{14,0},{1,15},{3,13... | collective-permute-start | bytes 147464 | tf_op jit(solution)/shard_map/ppermute | solution.py:31
  31.3 5.6 %collective-permute-start.13 = (bf16[32,1536]{1,0:T(8,128)(2,1)S(1)}, bf16[32,1536]{1,0:T(8,128)(2,1)S(1)}, u32[]{:S(2)}, u32[]{:S(2)}) collective-permute-start(bf16[32,1536]{1,0:T(8,128)(2,1)S(1)} %mix.7.refs_0_.refs_11_), channel_id=1, source_target_pairs={{0,1},{1,0},{2,3},{3,2},{4,5},{5,4},{6,7},{7,6},{8,9},{9,8},{10,11... | collective-permute-start | bytes 294920 | tf_op jit(solution)/shard_map/ppermute | solution.py:31
  33.3 7.0 %collective-permute-start.11 = (bf16[32,1536]{1,0:T(8,128)(2,1)S(1)}, bf16[32,1536]{1,0:T(8,128)(2,1)S(1)}, u32[]{:S(2)}, u32[]{:S(2)}) collective-permute-start(bf16[32,1536]{1,0:T(8,128)(2,1)S(1)} %mix.6.refs_0_.refs_8_), channel_id=1, source_target_pairs={{0,1},{1,0},{2,3},{3,2},{4,5},{5,4},{6,7},{7,6},{8,9},{9,8},{10,11... | collective-permute-start | bytes 294920 | tf_op jit(solution)/shard_map/ppermute | solution.py:31
  34.3 11.7 %collective-permute-start.7 = (bf16[32,1536]{1,0:T(8,128)(2,1)S(1)}, bf16[32,1536]{1,0:T(8,128)(2,1)S(1)}, u32[]{:S(2)}, u32[]{:S(2)}) collective-permute-start(bf16[32,1536]{1,0:T(8,128)(2,1)S(1)} %mix.4.refs_0_.refs_2_), channel_id=1, source_target_pairs={{0,1},{1,0},{2,3},{3,2},{4,5},{5,4},{6,7},{7,6},{8,9},{9,8},{10,11... | collective-permute-start | bytes 294920 | tf_op jit(solution)/shard_map/ppermute | solution.py:31
  36.3 6.4 %collective-permute-start.9 = (bf16[32,1536]{1,0:T(8,128)(2,1)S(1)}, bf16[32,1536]{1,0:T(8,128)(2,1)S(1)}, u32[]{:S(2)}, u32[]{:S(2)}) collective-permute-start(bf16[32,1536]{1,0:T(8,128)(2,1)S(1)} %mix.5.refs_0_.refs_5_), channel_id=1, source_target_pairs={{0,1},{1,0},{2,3},{3,2},{4,5},{5,4},{6,7},{7,6},{8,9},{9,8},{10,11... | collective-permute-start | bytes 294920 | tf_op jit(solution)/shard_map/ppermute | solution.py:31
  38.8 9.6 %collective-permute-start.14 = (bf16[32,1536]{1,0:T(8,128)(2,1)S(1)}, bf16[32,1536]{1,0:T(8,128)(2,1)S(1)}, u32[]{:S(2)}, u32[]{:S(2)}) collective-permute-start(bf16[32,1536]{1,0:T(8,128)(2,1)S(1)} %get-tuple-element.36), channel_id=1, source_target_pairs={{0,1},{1,0},{2,3},{3,2},{4,5},{5,4},{6,7},{7,6},{8,9},{9,8},{10,11... | collective-permute-start | bytes 294920 | tf_op jit(solution)/shard_map/ppermute | solution.py:31
  42.1 6.3 %collective-permute-start.12 = (bf16[32,1536]{1,0:T(8,128)(2,1)S(1)}, bf16[32,1536]{1,0:T(8,128)(2,1)S(1)}, u32[]{:S(2)}, u32[]{:S(2)}) collective-permute-start(bf16[32,1536]{1,0:T(8,128)(2,1)S(1)} %get-tuple-element.34), channel_id=1, source_target_pairs={{0,1},{1,0},{2,3},{3,2},{4,5},{5,4},{6,7},{7,6},{8,9},{9,8},{10,11... | collective-permute-start | bytes 294920 | tf_op jit(solution)/shard_map/ppermute | solution.py:31
  44.4 3.9 %copy-start.1 = (f32[1536]{0:T(1024)S(1)}, f32[1536]{0:T(1024)}, u32[]{:S(2)}) copy-start(f32[1536]{0:T(1024)} %param.15) | copy-start | bytes 18436
  44.5 4.7 %collective-permute-start.10 = (bf16[32,1536]{1,0:T(8,128)(2,1)S(1)}, bf16[32,1536]{1,0:T(8,128)(2,1)S(1)}, u32[]{:S(2)}, u32[]{:S(2)}) collective-permute-start(bf16[32,1536]{1,0:T(8,128)(2,1)S(1)} %get-tuple-element.32), channel_id=1, source_target_pairs={{0,1},{1,0},{2,3},{3,2},{4,5},{5,4},{6,7},{7,6},{8,9},{9,8},{10,11... | collective-permute-start | bytes 294920 | tf_op jit(solution)/shard_map/ppermute | solution.py:31
  47.8 4.7 %collective-permute-start.8 = (bf16[32,1536]{1,0:T(8,128)(2,1)S(1)}, bf16[32,1536]{1,0:T(8,128)(2,1)S(1)}, u32[]{:S(2)}, u32[]{:S(2)}) collective-permute-start(bf16[32,1536]{1,0:T(8,128)(2,1)S(1)} %get-tuple-element.30), channel_id=1, source_target_pairs={{0,1},{1,0},{2,3},{3,2},{4,5},{5,4},{6,7},{7,6},{8,9},{9,8},{10,11... | collective-permute-start | bytes 294920 | tf_op jit(solution)/shard_map/ppermute | solution.py:31
where the time goes:
time: 54 us; the launch traced here: 53.8 us
  Pallas kernels  21.2 us (39%)
  starting transfers between devices  21.1 us (39%)
  waiting for transfers between devices  11.1 us (21%)
    ppermute x15, starting transfers between devices, exchange(): lax.ppermute(value, axis, [(a, peer_of(a, step, count)) for a in range(co...  21.1 us
    ppermute x15, waiting for transfers between devices, exchange(): lax.ppermute(value, axis, [(a, peer_of(a, step, count)) for a in range(co...  11.1 us
    pallas_call x1, Pallas kernels, attention(): pl.pallas_call(lambda *refs: attention_kernel((tokens, heads, requests, h...  11.1 us
    pallas_call x4, Pallas kernels, ffn(): pl.pallas_call(lambda *refs: ffn_kernel((j, peers), *refs), out_shape=[ja...  7.01 us
    pallas_call x4, Pallas kernels, mix(): pl.pallas_call(lambda *refs: mix_kernel((tokens, heads, requests, width /...  1.72 us
    pallas_call x1, Pallas kernels, finish(): pl.pallas_call(lambda *refs: finish_kernel((heads, parts), *refs), out_sh...  1.32 us
  transfers between devices with their start and end apart: 15, of which 4 were waited for; matrix products, arithmetic and copies ran while one was open for 0% of the time, Pallas kernels for 15%

commit v1 on v0

--- a/solution.py
+++ b/solution.py
@@ -33,7 +33,7 @@
 
 def attention_kernel(sizes, len_hbm, query_hbm, key_hbm, value_hbm, *rest):
     tokens, heads, requests, head_size, positions, slots = sizes
-    send, len_ref, query_ref, key_buf, value_buf, query_f32, query_diag, first_ref, sems, small = rest
+    send, len_ref, query_ref, key_buf, value_buf, query_f32, query_diag, score_buf, first_ref, sems, small = rest
     width = heads * head_size
     lane_tiles = send.shape[0]
     blocks = requests // BLOCK_REQUESTS
@@ -51,7 +51,7 @@
     query_copy = pltpu.make_async_copy(query_hbm, query_ref, small.at[1])
     len_copy.start()
     query_copy.start()
-    for block in range(blocks):
+    for block in range(min(3, blocks)):
         for copy in copies(block):
             copy.start()
     len_copy.wait()
@@ -79,19 +79,37 @@
     factor = math.log2(math.e) * head_size ** (-0.5)
     lane = lax.broadcasted_iota(jnp.int32, (1, depth * positions), 1)
 
-    def block_body(block, carry):
-        for copy in copies(block):
-            copy.wait()
+    def spans(block):
         last = (block + 1) * chunk - 1
         for offset in range(BLOCK_REQUESTS):
             r = block * BLOCK_REQUESTS + offset
             first = first_ref[r]
+            yield offset, r, [jnp.minimum(first + b, last) for b in range(depth)]
+
+    def score(block):
+        for offset, r, index in spans(block):
+            keys = jnp.concatenate([key_buf[n] for n in index], axis=1)
+            score_buf[block % 2, offset] = jnp.dot(
+                queries, keys, preferred_element_type=jnp.float32
+            )
+
+    def block_body(block, carry):
+        following = jnp.minimum(block + 1, blocks - 1)
+
+        @pl.when(block + 1 < blocks)
+        def _():
+            for copy in copies(block + 1):
+                copy.wait()
+
+        @pl.when(block + 3 < blocks)
+        def _():
+            for copy in copies(block + 3):
+                copy.start()
+
+        for offset, r, index in spans(block):
             length = len_ref[base + r]
-            index = [jnp.minimum(first + b, last) for b in range(depth)]
-            keys = jnp.concatenate([key_buf[n] for n in index], axis=1)
             values = jnp.concatenate([value_buf[n] for n in index], axis=1)
-            scores = jnp.dot(queries, keys, preferred_element_type=jnp.float32)
-            scores = jnp.where(lane < length, scores, NEGATIVE_FILL)
+            scores = jnp.where(lane < length, score_buf[block % 2, offset], NEGATIVE_FILL)
             top = jnp.max(scores, axis=1, keepdims=True)
             terms = jnp.exp2((scores - top) * factor)
             total = jnp.sum(terms, axis=1, keepdims=True)
@@ -112,21 +130,26 @@
                 if spare:
                     kept = jnp.concatenate([kept, jnp.zeros((tokens, spare), jnp.float32)], axis=1)
                 for tile in range(lane_tiles):
-                    send[tile, pl.ds(i * requests + r, tokens, stride=heads * requests), :] = kept[
+                    send[tile, pl.ds(i * requests + r, tokens, stride=send.shape[1] // tokens), :] = kept[
                         :, tile * 128 : (tile + 1) * 128
                     ]
+        score(following)
         return carry
 
+    for copy in copies(0):
+        copy.wait()
+    score(0)
     lax.fori_loop(0, blocks, block_body, jnp.int32(0))
 
 
 def pack_kernel(sizes, send, *outs):
     tokens, rows, width = sizes
     lane_tiles = send.shape[0]
+    pitch = send.shape[1] // tokens
     mine = lax.axis_index("token")
     for out, step in zip(outs, message_order(tokens)):
         d = peer_of(mine, step, tokens)
-        where = pl.ds(pl.multiple_of(d * rows, rows), rows)
+        where = pl.ds(pl.multiple_of(d * pitch, 8), rows)
         values = jnp.concatenate([send[tile, where, :] for tile in range(lane_tiles)], axis=1)
         out[...] = values[:, :width].astype(jnp.bfloat16)
 
@@ -160,7 +183,9 @@
     flops = 4 * requests * LONGEST * heads * heads * tokens * width
     return pl.pallas_call(
         lambda *refs: attention_kernel((tokens, heads, requests, head_size, positions, slots), *refs),
-        out_shape=jax.ShapeDtypeStruct((lane_tiles, tokens * heads * requests, 128), jnp.float32),
+        out_shape=jax.ShapeDtypeStruct(
+            (lane_tiles, tokens * (heads * requests + 8), 128), jnp.float32
+        ),
         in_specs=[pl.BlockSpec(memory_space=pltpu.MemorySpace.HBM)] * 4,
         out_specs=pl.BlockSpec(memory_space=pltpu.VMEM),
         scratch_shapes=[
@@ -170,6 +195,10 @@
             pltpu.VMEM(values.shape, values.dtype),
             pltpu.VMEM(queries.shape, jnp.float32),
             pltpu.VMEM((heads * heads * tokens, width), jnp.float32),
+            pltpu.VMEM(
+                (2, BLOCK_REQUESTS, heads * heads * tokens, -(-LONGEST // positions) * positions),
+                jnp.float32,
+            ),
             pltpu.SMEM((requests,), jnp.int32),
             pltpu.SemaphoreType.DMA((2, blocks)),
             pltpu.SemaphoreType.DMA((2,)),

time: 54 us -> 51.3 us (0.950)
  Pallas kernels: 21.2 us -> 18.5 us
    pallas_call x1, Pallas kernels: 11.1 us -> 8.38 us  [attention(): pl.pallas_call(lambda *refs: attention_kernel((tokens, heads, requests, h...]
  transfers between devices with their start and end apart: 15 -> 15, of which waited for: 4 -> 4; matrix products, arithmetic and copies ran while one was open for 0% -> 0% of each run, Pallas kernels for 15% -> 16%
where the time goes in v1:
time: 51.3 us; the launch traced here: 51.1 us
  starting transfers between devices  21.2 us (41%)
  Pallas kernels  18.5 us (36%)
  waiting for transfers between devices  11.1 us (22%)
    ppermute x15, starting transfers between devices, exchange(): lax.ppermute(value, axis, [(a, peer_of(a, step, count)) for a in range(co...  21.2 us
    ppermute x15, waiting for transfers between devices, exchange(): lax.ppermute(value, axis, [(a, peer_of(a, step, count)) for a in range(co...  11.1 us
    pallas_call x1, Pallas kernels, attention(): pl.pallas_call(lambda *refs: attention_kernel((tokens, heads, requests, h...  8.38 us
    pallas_call x4, Pallas kernels, ffn(): pl.pallas_call(lambda *refs: ffn_kernel((j, peers), *refs), out_shape=[ja...  7.01 us
    pallas_call x4, Pallas kernels, mix(): pl.pallas_call(lambda *refs: mix_kernel((tokens, heads, requests, width /...  1.72 us
    pallas_call x1, Pallas kernels, finish(): pl.pallas_call(lambda *refs: finish_kernel((heads, parts), *refs), out_sh...  1.32 us
  transfers between devices with their start and end apart: 15, of which 4 were waited for; matrix products, arithmetic and copies ran while one was open for 0% of the time, Pallas kernels for 16%

profile of v1, /device:TPU:0, one launch (start us, length us, event | category | flops | bytes accessed | tf_op | source)
XLA Modules:
  0.0 51.1 jit_solution(9172954709704596174)
XLA Ops:
  0.0 8.4 %attention.1.refs_0_ = f32[2,1088,128]{2,1,0:T(8,128)S(1)} custom-call(s32[128]{0:T(128)} %refs_0_.1, bf16[32,192]{1,0:T(8,128)(2,1)} %refs_1_.1, bf16[96,192,128]{2,1,0:T(8,128)(2,1)} %refs_2_.5, bf16[96,192,128]{2,1,0:T(8,128)(2,1)} %refs_3_.5), custom_call_target="tpu_custom_call" | custom-call | flops 1610612736 | bytes 9437184 | tf_op jit(solution)/shard_map/attention/pallas_call | solution.py:184
  8.4 0.0 copy-start
  8.4 0.0 slice-start.1
  8.5 0.0 slice-start.6
  8.5 0.1 pack.1
  8.6 3.0 %collective-permute-start = (bf16[128,192]{1,0:T(8,128)(2,1)S(1)}, bf16[128,192]{1,0:T(8,128)(2,1)S(1)}, u32[]{:S(2)}, u32[]{:S(2)}) collective-permute-start(bf16[128,192]{1,0:T(8,128)(2,1)S(1)} %get-tuple-element.22.refs_1_), channel_id=1, source_target_pairs={{0,2},{2,0},{4,6},{6,4},{8,10},{10,8},{12,14},{14,12},{1,3},{3,1},... | collective-permute-start | bytes 147464 | tf_op jit(solution)/shard_map/ppermute | solution.py:31
  11.6 1.6 %collective-permute-start.1 = (bf16[128,192]{1,0:T(8,128)(2,1)S(1)}, bf16[128,192]{1,0:T(8,128)(2,1)S(1)}, u32[]{:S(2)}, u32[]{:S(2)}) collective-permute-start(bf16[128,192]{1,0:T(8,128)(2,1)S(1)} %get-tuple-element.23.refs_2_), channel_id=1, source_target_pairs={{0,4},{2,6},{4,0},{6,2},{8,12},{10,14},{12,8},{14,10},{1,5},{3,7},... | collective-permute-start | bytes 147464 | tf_op jit(solution)/shard_map/ppermute | solution.py:31
  13.2 3.0 %collective-permute-start.3 = (bf16[128,192]{1,0:T(8,128)(2,1)S(1)}, bf16[128,192]{1,0:T(8,128)(2,1)S(1)}, u32[]{:S(2)}, u32[]{:S(2)}) collective-permute-start(bf16[128,192]{1,0:T(8,128)(2,1)S(1)} %get-tuple-element.25.refs_4_), channel_id=1, source_target_pairs={{0,8},{2,10},{4,12},{6,14},{8,0},{10,2},{12,4},{14,6},{1,9},{3,11}... | collective-permute-start | bytes 147464 | tf_op jit(solution)/shard_map/ppermute | solution.py:31
  16.2 1.3 %collective-permute-start.4 = (bf16[128,192]{1,0:T(8,128)(2,1)S(1)}, bf16[128,192]{1,0:T(8,128)(2,1)S(1)}, u32[]{:S(2)}, u32[]{:S(2)}) collective-permute-start(bf16[128,192]{1,0:T(8,128)(2,1)S(1)} %get-tuple-element.26.refs_5_), channel_id=1, source_target_pairs={{0,10},{2,8},{4,14},{6,12},{8,2},{10,0},{12,6},{14,4},{1,11},{3,9}... | collective-permute-start | bytes 147464 | tf_op jit(solution)/shard_map/ppermute | solution.py:31
  17.5 3.6 %collective-permute-start.5 = (bf16[128,192]{1,0:T(8,128)(2,1)S(1)}, bf16[128,192]{1,0:T(8,128)(2,1)S(1)}, u32[]{:S(2)}, u32[]{:S(2)}) collective-permute-start(bf16[128,192]{1,0:T(8,128)(2,1)S(1)} %get-tuple-element.27.refs_6_), channel_id=1, source_target_pairs={{0,12},{2,14},{4,8},{6,10},{8,4},{10,6},{12,0},{14,2},{1,13},{3,15... | collective-permute-start | bytes 147464 | tf_op jit(solution)/shard_map/ppermute | solution.py:31
  21.1 0.0 collective-permute-start.6
  21.1 5.2 %collective-permute-done.4.refs_13_ = bf16[128,192]{1,0:T(8,128)(2,1)S(1)} collective-permute-done((bf16[128,192]{1,0:T(8,128)(2,1)S(1)}, bf16[128,192]{1,0:T(8,128)(2,1)S(1)}, u32[]{:S(2)}, u32[]{:S(2)}) %collective-permute-start.4) | collective-permute-done | bytes 49184 | tf_op jit(solution)/shard_map/ppermute | solution.py:31
  26.4 1.7 %collective-permute-done.6.refs_15_ = bf16[128,192]{1,0:T(8,128)(2,1)S(1)} collective-permute-done((bf16[128,192]{1,0:T(8,128)(2,1)S(1)}, bf16[128,192]{1,0:T(8,128)(2,1)S(1)}, u32[]{:S(2)}, u32[]{:S(2)}) %collective-permute-start.6) | collective-permute-done | bytes 49184 | tf_op jit(solution)/shard_map/ppermute | solution.py:31
  28.1 0.4 mix.7.refs_0_.refs_11_
  28.6 1.6 %collective-permute-start.13 = (bf16[32,1536]{1,0:T(8,128)(2,1)S(1)}, bf16[32,1536]{1,0:T(8,128)(2,1)S(1)}, u32[]{:S(2)}, u32[]{:S(2)}) collective-permute-start(bf16[32,1536]{1,0:T(8,128)(2,1)S(1)} %mix.7.refs_0_.refs_11_), channel_id=1, source_target_pairs={{0,1},{1,0},{2,3},{3,2},{4,5},{5,4},{6,7},{7,6},{8,9},{9,8},{10,11... | collective-permute-start | bytes 294920 | tf_op jit(solution)/shard_map/ppermute | solution.py:31
  30.2 0.5 mix.6.refs_0_.refs_8_
  30.6 0.5 %collective-permute-start.11 = (bf16[32,1536]{1,0:T(8,128)(2,1)S(1)}, bf16[32,1536]{1,0:T(8,128)(2,1)S(1)}, u32[]{:S(2)}, u32[]{:S(2)}) collective-permute-start(bf16[32,1536]{1,0:T(8,128)(2,1)S(1)} %mix.6.refs_0_.refs_8_), channel_id=1, source_target_pairs={{0,1},{1,0},{2,3},{3,2},{4,5},{5,4},{6,7},{7,6},{8,9},{9,8},{10,11... | collective-permute-start | bytes 294920 | tf_op jit(solution)/shard_map/ppermute | solution.py:31
  31.2 0.4 mix.4.refs_0_.refs_2_
  31.6 1.6 %collective-permute-start.7 = (bf16[32,1536]{1,0:T(8,128)(2,1)S(1)}, bf16[32,1536]{1,0:T(8,128)(2,1)S(1)}, u32[]{:S(2)}, u32[]{:S(2)}) collective-permute-start(bf16[32,1536]{1,0:T(8,128)(2,1)S(1)} %mix.4.refs_0_.refs_2_), channel_id=1, source_target_pairs={{0,1},{1,0},{2,3},{3,2},{4,5},{5,4},{6,7},{7,6},{8,9},{9,8},{10,11... | collective-permute-start | bytes 294920 | tf_op jit(solution)/shard_map/ppermute | solution.py:31
  33.2 0.4 mix.5.refs_0_.refs_5_
  33.7 0.5 %collective-permute-start.9 = (bf16[32,1536]{1,0:T(8,128)(2,1)S(1)}, bf16[32,1536]{1,0:T(8,128)(2,1)S(1)}, u32[]{:S(2)}, u32[]{:S(2)}) collective-permute-start(bf16[32,1536]{1,0:T(8,128)(2,1)S(1)} %mix.5.refs_0_.refs_5_), channel_id=1, source_target_pairs={{0,1},{1,0},{2,3},{3,2},{4,5},{5,4},{6,7},{7,6},{8,9},{9,8},{10,11... | collective-permute-start | bytes 294920 | tf_op jit(solution)/shard_map/ppermute | solution.py:31
  34.3 1.8 %ffn.7 = (f32[32,1536]{1,0:T(8,128)S(1)}, bf16[32,1536]{1,0:T(8,128)(2,1)S(1)}) custom-call(bf16[32,1536]{1,0:T(8,128)(2,1)S(1)} %mix.7.refs_0_.refs_11_, bf16[32,1536]{1,0:T(8,128)(2,1)S(1)} %collective-permute-done.13.refs_1_, bf16[4,1536,1536]{2,1,0:T(8,128)(2,1)S(1)} %bitcast.1, bf16[4,1536,1536]{2,1,0:T(8,128)(2,1)S(1)} %bitcast.3), custom_call_target="tpu_custom_call" | custom-call | flops 603979776 | bytes 9437184 | tf_op jit(solution)/shard_map/ffn/pallas_call | solution.py:283
  36.1 1.6 %collective-permute-start.14 = (bf16[32,1536]{1,0:T(8,128)(2,1)S(1)}, bf16[32,1536]{1,0:T(8,128)(2,1)S(1)}, u32[]{:S(2)}, u32[]{:S(2)}) collective-permute-start(bf16[32,1536]{1,0:T(8,128)(2,1)S(1)} %get-tuple-element.36), channel_id=1, source_target_pairs={{0,1},{1,0},{2,3},{3,2},{4,5},{5,4},{6,7},{7,6},{8,9},{9,8},{10,11... | collective-permute-start | bytes 294920 | tf_op jit(solution)/shard_map/ppermute | solution.py:31
  37.7 1.8 %ffn.6 = (f32[32,1536]{1,0:T(8,128)S(1)}, bf16[32,1536]{1,0:T(8,128)(2,1)S(1)}) custom-call(bf16[32,1536]{1,0:T(8,128)(2,1)S(1)} %mix.6.refs_0_.refs_8_, bf16[32,1536]{1,0:T(8,128)(2,1)S(1)} %collective-permute-done.11.refs_1_, bf16[4,1536,1536]{2,1,0:T(8,128)(2,1)S(1)} %bitcast.1, bf16[4,1536,1536]{2,1,0:T(8,128)(2,1)S(1)} %bitcast.3), custom_call_target="tpu_custom_call" | custom-call | flops 603979776 | bytes 9437184 | tf_op jit(solution)/shard_map/ffn/pallas_call | solution.py:283
  39.4 0.5 %collective-permute-start.12 = (bf16[32,1536]{1,0:T(8,128)(2,1)S(1)}, bf16[32,1536]{1,0:T(8,128)(2,1)S(1)}, u32[]{:S(2)}, u32[]{:S(2)}) collective-permute-start(bf16[32,1536]{1,0:T(8,128)(2,1)S(1)} %get-tuple-element.34), channel_id=1, source_target_pairs={{0,1},{1,0},{2,3},{3,2},{4,5},{5,4},{6,7},{7,6},{8,9},{9,8},{10,11... | collective-permute-start | bytes 294920 | tf_op jit(solution)/shard_map/ppermute | solution.py:31
  40.0 1.8 %ffn.5 = (f32[32,1536]{1,0:T(8,128)S(1)}, bf16[32,1536]{1,0:T(8,128)(2,1)S(1)}) custom-call(bf16[32,1536]{1,0:T(8,128)(2,1)S(1)} %mix.5.refs_0_.refs_5_, bf16[32,1536]{1,0:T(8,128)(2,1)S(1)} %collective-permute-done.9.refs_1_, bf16[4,1536,1536]{2,1,0:T(8,128)(2,1)S(1)} %bitcast.1, bf16[4,1536,1536]{2,1,0:T(8,128)(2,1)S(1)} %bitcast.3), custom_call_target="tpu_custom_call" | custom-call | flops 603979776 | bytes 9437184 | tf_op jit(solution)/shard_map/ffn/pallas_call | solution.py:283
  41.8 1.6 %collective-permute-start.10 = (bf16[32,1536]{1,0:T(8,128)(2,1)S(1)}, bf16[32,1536]{1,0:T(8,128)(2,1)S(1)}, u32[]{:S(2)}, u32[]{:S(2)}) collective-permute-start(bf16[32,1536]{1,0:T(8,128)(2,1)S(1)} %get-tuple-element.32), channel_id=1, source_target_pairs={{0,1},{1,0},{2,3},{3,2},{4,5},{5,4},{6,7},{7,6},{8,9},{9,8},{10,11... | collective-permute-start | bytes 294920 | tf_op jit(solution)/shard_map/ppermute | solution.py:31
  43.4 1.8 %ffn.4 = (f32[32,1536]{1,0:T(8,128)S(1)}, bf16[32,1536]{1,0:T(8,128)(2,1)S(1)}) custom-call(bf16[32,1536]{1,0:T(8,128)(2,1)S(1)} %mix.4.refs_0_.refs_2_, bf16[32,1536]{1,0:T(8,128)(2,1)S(1)} %collective-permute-done.7.refs_1_, bf16[4,1536,1536]{2,1,0:T(8,128)(2,1)S(1)} %bitcast.1, bf16[4,1536,1536]{2,1,0:T(8,128)(2,1)S(1)} %bitcast.3), custom_call_target="tpu_custom_call" | custom-call | flops 603979776 | bytes 9437184 | tf_op jit(solution)/shard_map/ffn/pallas_call | solution.py:283
  45.1 0.5 %collective-permute-start.8 = (bf16[32,1536]{1,0:T(8,128)(2,1)S(1)}, bf16[32,1536]{1,0:T(8,128)(2,1)S(1)}, u32[]{:S(2)}, u32[]{:S(2)}) collective-permute-start(bf16[32,1536]{1,0:T(8,128)(2,1)S(1)} %get-tuple-element.30), channel_id=1, source_target_pairs={{0,1},{1,0},{2,3},{3,2},{4,5},{5,4},{6,7},{7,6},{8,9},{9,8},{10,11... | collective-permute-start | bytes 294920 | tf_op jit(solution)/shard_map/ppermute | solution.py:31
  45.7 0.7 %collective-permute-done.10.refs_4_ = bf16[32,1536]{1,0:T(8,128)(2,1)S(1)} collective-permute-done((bf16[32,1536]{1,0:T(8,128)(2,1)S(1)}, bf16[32,1536]{1,0:T(8,128)(2,1)S(1)}, u32[]{:S(2)}, u32[]{:S(2)}) %collective-permute-start.10) | collective-permute-done | bytes 98336 | tf_op jit(solution)/shard_map/ppermute | solution.py:31
  46.4 3.4 %collective-permute-done.8.refs_1_ = bf16[32,1536]{1,0:T(8,128)(2,1)S(1)} collective-permute-done((bf16[32,1536]{1,0:T(8,128)(2,1)S(1)}, bf16[32,1536]{1,0:T(8,128)(2,1)S(1)}, u32[]{:S(2)}, u32[]{:S(2)}) %collective-permute-start.8) | collective-permute-done | bytes 98336 | tf_op jit(solution)/shard_map/ppermute | solution.py:31
  49.8 1.3 %finish.1 = bf16[32,4,1536]{2,1,0:T(4,128)(2,1)} custom-call(f32[32,1536]{1,0:T(8,128)S(1)} %get-tuple-element.29.refs_0_, bf16[32,1536]{1,0:T(8,128)(2,1)S(1)} %collective-permute-done.8.refs_1_, bf16[32,1536]{1,0:T(8,128)(2,1)S(1)} %mix.4.refs_0_.refs_2_, f32[32,1536]{1,0:T(8,128)S(1)} %get-tuple-element.31.refs_3_, ...), custom_call_target="tpu_custom_call" | custom-call | flops 1966080 | bytes 1572864 | tf_op jit(solution)/shard_map/finish/pallas_call | solution.py:314
  (37 shorter events, 0.1 us)
Async XLA Ops:
  0.0 34.2 %slice-start = ((s8[18874368]{0:T(1024)(128)(4,1)}), s8[4194304]{0:T(1024)(128)(4,1)S(1)}, s32[]{:S(2)}) async-start(s8[18874368]{0:T(1024)(128)(4,1)} %bitcast), calls=%async_computation | async-start | bytes 8388608
  0.0 34.2 %slice-start.5 = ((s8[18874368]{0:T(1024)(128)(4,1)}), s8[2097152]{0:T(1024)(128)(4,1)S(1)}, s32[]{:S(2)}) async-start(s8[18874368]{0:T(1024)(128)(4,1)} %bitcast.2), calls=%async_computation.5 | async-start | bytes 4194304
  8.4 12.7 %copy-start = (f32[1536]{0:T(1024)S(1)}, f32[1536]{0:T(1024)}, u32[]{:S(2)}) copy-start(f32[1536]{0:T(1024)} %param.12) | copy-start | bytes 18436
  8.4 25.8 %slice-start.1 = ((s8[18874368]{0:T(1024)(128)(4,1)}), s8[4194304]{0:T(1024)(128)(4,1)S(1)}, s32[]{:S(2)}) async-start(s8[18874368]{0:T(1024)(128)(4,1)} %bitcast), calls=%async_computation.1 | async-start | bytes 8388608
  8.4 25.8 %slice-start.2 = ((s8[18874368]{0:T(1024)(128)(4,1)}), s8[4194304]{0:T(1024)(128)(4,1)S(1)}, s32[]{:S(2)}) async-start(s8[18874368]{0:T(1024)(128)(4,1)} %bitcast), calls=%async_computation.2 | async-start | bytes 8388608
  8.4 25.8 %slice-start.3 = ((s8[18874368]{0:T(1024)(128)(4,1)}), s8[4194304]{0:T(1024)(128)(4,1)S(1)}, s32[]{:S(2)}) async-start(s8[18874368]{0:T(1024)(128)(4,1)} %bitcast), calls=%async_computation.3 | async-start | bytes 8388608
  8.4 25.8 %slice-start.4 = ((s8[18874368]{0:T(1024)(128)(4,1)}), s8[2097152]{0:T(1024)(128)(4,1)S(1)}, s32[]{:S(2)}) async-start(s8[18874368]{0:T(1024)(128)(4,1)} %bitcast), calls=%async_computation.4 | async-start | bytes 4194304
  8.5 25.8 %slice-start.6 = ((s8[18874368]{0:T(1024)(128)(4,1)}), s8[4194304]{0:T(1024)(128)(4,1)S(1)}, s32[]{:S(2)}) async-start(s8[18874368]{0:T(1024)(128)(4,1)} %bitcast.2), calls=%async_computation.6 | async-start | bytes 8388608
  8.5 25.8 %slice-start.7 = ((s8[18874368]{0:T(1024)(128)(4,1)}), s8[4194304]{0:T(1024)(128)(4,1)S(1)}, s32[]{:S(2)}) async-start(s8[18874368]{0:T(1024)(128)(4,1)} %bitcast.2), calls=%async_computation.7 | async-start | bytes 8388608
  8.5 25.8 %slice-start.8 = ((s8[18874368]{0:T(1024)(128)(4,1)}), s8[4194304]{0:T(1024)(128)(4,1)S(1)}, s32[]{:S(2)}) async-start(s8[18874368]{0:T(1024)(128)(4,1)} %bitcast.2), calls=%async_computation.8 | async-start | bytes 8388608
  8.5 25.8 %slice-start.9 = ((s8[18874368]{0:T(1024)(128)(4,1)}), s8[4194304]{0:T(1024)(128)(4,1)S(1)}, s32[]{:S(2)}) async-start(s8[18874368]{0:T(1024)(128)(4,1)} %bitcast.2), calls=%async_computation.9 | async-start | bytes 8388608
  8.6 8.9 %collective-permute-start = (bf16[128,192]{1,0:T(8,128)(2,1)S(1)}, bf16[128,192]{1,0:T(8,128)(2,1)S(1)}, u32[]{:S(2)}, u32[]{:S(2)}) collective-permute-start(bf16[128,192]{1,0:T(8,128)(2,1)S(1)} %get-tuple-element.22.refs_1_), channel_id=1, source_target_pairs={{0,2},{2,0},{4,6},{6,4},{8,10},{10,8},{12,14},{14,12},{1,3},{3,1},... | collective-permute-start | bytes 147464 | tf_op jit(solution)/shard_map/ppermute | solution.py:31
  11.6 9.5 %collective-permute-start.1 = (bf16[128,192]{1,0:T(8,128)(2,1)S(1)}, bf16[128,192]{1,0:T(8,128)(2,1)S(1)}, u32[]{:S(2)}, u32[]{:S(2)}) collective-permute-start(bf16[128,192]{1,0:T(8,128)(2,1)S(1)} %get-tuple-element.23.refs_2_), channel_id=1, source_target_pairs={{0,4},{2,6},{4,0},{6,2},{8,12},{10,14},{12,8},{14,10},{1,5},{3,7},... | collective-permute-start | bytes 147464 | tf_op jit(solution)/shard_map/ppermute | solution.py:31
  13.2 7.9 %collective-permute-start.2 = (bf16[128,192]{1,0:T(8,128)(2,1)S(1)}, bf16[128,192]{1,0:T(8,128)(2,1)S(1)}, u32[]{:S(2)}, u32[]{:S(2)}) collective-permute-start(bf16[128,192]{1,0:T(8,128)(2,1)S(1)} %get-tuple-element.24.refs_3_), channel_id=1, source_target_pairs={{0,6},{2,4},{4,2},{6,0},{8,14},{10,12},{12,10},{14,8},{1,7},{3,5},... | collective-permute-start | bytes 147464 | tf_op jit(solution)/shard_map/ppermute | solution.py:31
  13.2 7.9 %collective-permute-start.3 = (bf16[128,192]{1,0:T(8,128)(2,1)S(1)}, bf16[128,192]{1,0:T(8,128)(2,1)S(1)}, u32[]{:S(2)}, u32[]{:S(2)}) collective-permute-start(bf16[128,192]{1,0:T(8,128)(2,1)S(1)} %get-tuple-element.25.refs_4_), channel_id=1, source_target_pairs={{0,8},{2,10},{4,12},{6,14},{8,0},{10,2},{12,4},{14,6},{1,9},{3,11}... | collective-permute-start | bytes 147464 | tf_op jit(solution)/shard_map/ppermute | solution.py:31
  16.2 10.2 %collective-permute-start.4 = (bf16[128,192]{1,0:T(8,128)(2,1)S(1)}, bf16[128,192]{1,0:T(8,128)(2,1)S(1)}, u32[]{:S(2)}, u32[]{:S(2)}) collective-permute-start(bf16[128,192]{1,0:T(8,128)(2,1)S(1)} %get-tuple-element.26.refs_5_), channel_id=1, source_target_pairs={{0,10},{2,8},{4,14},{6,12},{8,2},{10,0},{12,6},{14,4},{1,11},{3,9}... | collective-permute-start | bytes 147464 | tf_op jit(solution)/shard_map/ppermute | solution.py:31
  17.5 8.9 %collective-permute-start.5 = (bf16[128,192]{1,0:T(8,128)(2,1)S(1)}, bf16[128,192]{1,0:T(8,128)(2,1)S(1)}, u32[]{:S(2)}, u32[]{:S(2)}) collective-permute-start(bf16[128,192]{1,0:T(8,128)(2,1)S(1)} %get-tuple-element.27.refs_6_), channel_id=1, source_target_pairs={{0,12},{2,14},{4,8},{6,10},{8,4},{10,6},{12,0},{14,2},{1,13},{3,15... | collective-permute-start | bytes 147464 | tf_op jit(solution)/shard_map/ppermute | solution.py:31
  21.1 7.1 %collective-permute-start.6 = (bf16[128,192]{1,0:T(8,128)(2,1)S(1)}, bf16[128,192]{1,0:T(8,128)(2,1)S(1)}, u32[]{:S(2)}, u32[]{:S(2)}) collective-permute-start(bf16[128,192]{1,0:T(8,128)(2,1)S(1)} %get-tuple-element.28.refs_7_), channel_id=1, source_target_pairs={{0,14},{2,12},{4,10},{6,8},{8,6},{10,4},{12,2},{14,0},{1,15},{3,13... | collective-permute-start | bytes 147464 | tf_op jit(solution)/shard_map/ppermute | solution.py:31
  28.6 5.6 %collective-permute-start.13 = (bf16[32,1536]{1,0:T(8,128)(2,1)S(1)}, bf16[32,1536]{1,0:T(8,128)(2,1)S(1)}, u32[]{:S(2)}, u32[]{:S(2)}) collective-permute-start(bf16[32,1536]{1,0:T(8,128)(2,1)S(1)} %mix.7.refs_0_.refs_11_), channel_id=1, source_target_pairs={{0,1},{1,0},{2,3},{3,2},{4,5},{5,4},{6,7},{7,6},{8,9},{9,8},{10,11... | collective-permute-start | bytes 294920 | tf_op jit(solution)/shard_map/ppermute | solution.py:31
  30.6 7.0 %collective-permute-start.11 = (bf16[32,1536]{1,0:T(8,128)(2,1)S(1)}, bf16[32,1536]{1,0:T(8,128)(2,1)S(1)}, u32[]{:S(2)}, u32[]{:S(2)}) collective-permute-start(bf16[32,1536]{1,0:T(8,128)(2,1)S(1)} %mix.6.refs_0_.refs_8_), channel_id=1, source_target_pairs={{0,1},{1,0},{2,3},{3,2},{4,5},{5,4},{6,7},{7,6},{8,9},{9,8},{10,11... | collective-permute-start | bytes 294920 | tf_op jit(solution)/shard_map/ppermute | solution.py:31
  31.6 11.8 %collective-permute-start.7 = (bf16[32,1536]{1,0:T(8,128)(2,1)S(1)}, bf16[32,1536]{1,0:T(8,128)(2,1)S(1)}, u32[]{:S(2)}, u32[]{:S(2)}) collective-permute-start(bf16[32,1536]{1,0:T(8,128)(2,1)S(1)} %mix.4.refs_0_.refs_2_), channel_id=1, source_target_pairs={{0,1},{1,0},{2,3},{3,2},{4,5},{5,4},{6,7},{7,6},{8,9},{9,8},{10,11... | collective-permute-start | bytes 294920 | tf_op jit(solution)/shard_map/ppermute | solution.py:31
  33.7 6.3 %collective-permute-start.9 = (bf16[32,1536]{1,0:T(8,128)(2,1)S(1)}, bf16[32,1536]{1,0:T(8,128)(2,1)S(1)}, u32[]{:S(2)}, u32[]{:S(2)}) collective-permute-start(bf16[32,1536]{1,0:T(8,128)(2,1)S(1)} %mix.5.refs_0_.refs_5_), channel_id=1, source_target_pairs={{0,1},{1,0},{2,3},{3,2},{4,5},{5,4},{6,7},{7,6},{8,9},{9,8},{10,11... | collective-permute-start | bytes 294920 | tf_op jit(solution)/shard_map/ppermute | solution.py:31
  36.1 9.6 %collective-permute-start.14 = (bf16[32,1536]{1,0:T(8,128)(2,1)S(1)}, bf16[32,1536]{1,0:T(8,128)(2,1)S(1)}, u32[]{:S(2)}, u32[]{:S(2)}) collective-permute-start(bf16[32,1536]{1,0:T(8,128)(2,1)S(1)} %get-tuple-element.36), channel_id=1, source_target_pairs={{0,1},{1,0},{2,3},{3,2},{4,5},{5,4},{6,7},{7,6},{8,9},{9,8},{10,11... | collective-permute-start | bytes 294920 | tf_op jit(solution)/shard_map/ppermute | solution.py:31
  39.4 6.3 %collective-permute-start.12 = (bf16[32,1536]{1,0:T(8,128)(2,1)S(1)}, bf16[32,1536]{1,0:T(8,128)(2,1)S(1)}, u32[]{:S(2)}, u32[]{:S(2)}) collective-permute-start(bf16[32,1536]{1,0:T(8,128)(2,1)S(1)} %get-tuple-element.34), channel_id=1, source_target_pairs={{0,1},{1,0},{2,3},{3,2},{4,5},{5,4},{6,7},{7,6},{8,9},{9,8},{10,11... | collective-permute-start | bytes 294920 | tf_op jit(solution)/shard_map/ppermute | solution.py:31
  41.8 3.9 %copy-start.1 = (f32[1536]{0:T(1024)S(1)}, f32[1536]{0:T(1024)}, u32[]{:S(2)}) copy-start(f32[1536]{0:T(1024)} %param.15) | copy-start | bytes 18436
  41.8 4.7 %collective-permute-start.10 = (bf16[32,1536]{1,0:T(8,128)(2,1)S(1)}, bf16[32,1536]{1,0:T(8,128)(2,1)S(1)}, u32[]{:S(2)}, u32[]{:S(2)}) collective-permute-start(bf16[32,1536]{1,0:T(8,128)(2,1)S(1)} %get-tuple-element.32), channel_id=1, source_target_pairs={{0,1},{1,0},{2,3},{3,2},{4,5},{5,4},{6,7},{7,6},{8,9},{9,8},{10,11... | collective-permute-start | bytes 294920 | tf_op jit(solution)/shard_map/ppermute | solution.py:31
  45.1 4.7 %collective-permute-start.8 = (bf16[32,1536]{1,0:T(8,128)(2,1)S(1)}, bf16[32,1536]{1,0:T(8,128)(2,1)S(1)}, u32[]{:S(2)}, u32[]{:S(2)}) collective-permute-start(bf16[32,1536]{1,0:T(8,128)(2,1)S(1)} %get-tuple-element.30), channel_id=1, source_target_pairs={{0,1},{1,0},{2,3},{3,2},{4,5},{5,4},{6,7},{7,6},{8,9},{9,8},{10,11... | collective-permute-start | bytes 294920 | tf_op jit(solution)/shard_map/ppermute | solution.py:31

commit v2 on v1

--- a/solution.py
+++ b/solution.py
@@ -263,31 +263,33 @@
 
 
 def ffn_kernel(sizes, *refs):
-    j, peers = sizes
+    j, peers, place = sizes
     rows = refs[:peers]
     up_ref, down_ref = refs[peers : peers + 2]
-    outs = refs[peers + 2 :]
+    outs = refs[-peers:]
     x = jnp.concatenate([ref[...] for ref in rows], axis=0)
     lifted = jnp.dot(x, up_ref[j], preferred_element_type=jnp.float32)
     activated = (0.5 * lifted * (1.0 + lax.erf(lifted * math.sqrt(0.5)))).astype(jnp.bfloat16)
     total = jnp.dot(activated, down_ref[j], preferred_element_type=jnp.float32)
     count = rows[0].shape[0]
-    for k in range(peers):
-        outs[k][...] = total[k * count : (k + 1) * count].astype(outs[k].dtype)
-
-
-def ffn(rows, w_up, w_down, j):
+    outs[0][...] = total[:count]
+    for k in range(1, peers):
+        outs[k][place * count : (place + 1) * count, :] = total[k * count : (k + 1) * count].astype(
+            outs[k].dtype
+        )
+
+
+def ffn(rows, w_up, w_down, j, place, together, carried):
     _, model, hidden = w_up.shape
     peers = len(rows)
     count = rows[0].shape[0]
     return pl.pallas_call(
-        lambda *refs: ffn_kernel((j, peers), *refs),
-        out_shape=[
-            jax.ShapeDtypeStruct((count, model), jnp.float32 if k == 0 else jnp.bfloat16)
-            for k in range(peers)
-        ],
-        in_specs=[pl.BlockSpec(memory_space=pltpu.VMEM)] * (peers + 2),
+        lambda *refs: ffn_kernel((j, peers, place), *refs),
+        out_shape=[jax.ShapeDtypeStruct((count, model), jnp.float32)]
+        + [jax.ShapeDtypeStruct((together * count, model), jnp.bfloat16)] * (peers - 1),
+        in_specs=[pl.BlockSpec(memory_space=pltpu.VMEM)] * (peers + 2 + len(carried)),
         out_specs=[pl.BlockSpec(memory_space=pltpu.VMEM)] * peers,
+        input_output_aliases={peers + 2 + n: 1 + n for n in range(len(carried))},
         compiler_params=pltpu.CompilerParams(vmem_limit_bytes=8 * MIB),
         cost_estimate=pl.CostEstimate(
             flops=4 * peers * count * model * hidden,
@@ -295,31 +297,62 @@
             bytes_accessed=4 * model * hidden,
         ),
         name="ffn",
-    )(*rows, w_up, w_down)
-
-
-def finish_kernel(sizes, *refs):
-    heads, parts = sizes
-    gain_ref, out_ref = refs[heads * parts :]
-    for j in range(heads):
-        summed = refs[j * parts][...]
-        for ref in refs[j * parts + 1 : (j + 1) * parts]:
-            summed = summed + ref[...].astype(jnp.float32)
-        out_ref[:, j, :] = (norm_rows(summed) * gain_ref[...]).astype(jnp.bfloat16)
-
-
-def finish(terms, gain):
-    heads, parts = len(terms), len(terms[0])
-    count, model = terms[0][0].shape
-    return pl.pallas_call(
-        lambda *refs: finish_kernel((heads, parts), *refs),
-        out_shape=jax.ShapeDtypeStruct((count, heads, model), jnp.bfloat16),
-        compiler_params=pltpu.CompilerParams(vmem_limit_bytes=16 * MIB),
-        cost_estimate=pl.CostEstimate(
-            flops=10 * heads * count * model, transcendentals=0, bytes_accessed=8 * heads * count * model
-        ),
-        name="finish",
-    )(*[part for token in terms for part in token], gain)
+    )(*rows, w_up, w_down, *carried)
+
+
+def finished(own, normed, back, place, gain_ref):
+    count = own.shape[0]
+    summed = own[...] + normed[...].astype(jnp.float32)
+    for ref in back:
+        summed = summed + ref[place * count : (place + 1) * count, :].astype(jnp.float32)
+    return norm_rows(summed) * gain_ref[...]
+
+
+def finish_kernel(sizes, last, *refs):
+    together, done = sizes
+    own, normed = refs[:together], refs[together : 2 * together]
+    back = refs[2 * together : len(refs) - (1 if last else together) - 1 - done]
+    early = refs[2 * together + len(back) : 2 * together + len(back) + done]
+    gain_ref = refs[2 * together + len(back) + done]
+    outs = refs[2 * together + len(back) + done + 1 :]
+    if last:
+        for j, ref in enumerate(early):
+            outs[0][:, j, :] = ref[...].astype(jnp.bfloat16)
+    for place in range(together):
+        rows = finished(own[place], normed[place], back, place, gain_ref)
+        if last:
+            outs[0][:, done + place, :] = rows.astype(jnp.bfloat16)
+        else:
+            outs[place][...] = rows
+
+
+def finish(groups, gain):
+    done = []
+    for n, (own, normed, back) in enumerate(groups):
+        last = n == len(groups) - 1
+        together = len(own)
+        count, model = own[0].shape
+        early = done if last else []
+        if last:
+            shape = jax.ShapeDtypeStruct((count, len(done) + together, model), jnp.bfloat16)
+        else:
+            shape = [jax.ShapeDtypeStruct((count, model), jnp.float32)] * together
+        args = [*own, *normed, *back, *early, gain]
+        sizes = (together, len(early))
+        out = pl.pallas_call(
+            lambda *refs, sizes=sizes, last=last: finish_kernel(sizes, last, *refs),
+            out_shape=shape,
+            compiler_params=pltpu.CompilerParams(vmem_limit_bytes=16 * MIB),
+            cost_estimate=pl.CostEstimate(
+                flops=10 * together * count * model,
+                transcendentals=0,
+                bytes_accessed=8 * together * count * model,
+            ),
+            name="finish" if last else "finish_early",
+        )(*args)
+        if not last:
+            done.extend(out)
+    return out
 
 
 def local(hist_len, queries, history_keys, cached_history_values, gain_mix, w_up, w_down, gain_out):
@@ -340,15 +373,20 @@
     gain_mix = gain_mix.reshape(1, -1)
     gain_out = gain_out.reshape(1, -1)
     normed = [mix(sent, received, gain_mix, j, tokens, requests) for j in range(heads)]
-    terms = []
-    for j in range(heads):
-        rows = [normed[j]] + [exchange(normed[j], "hidden", k, sides) for k in range(1, sides)]
-        parts = ffn(rows, w_up, w_down, j)
+    together = 2 if heads % 2 == 0 else 1
+    groups = []
+    for start in range(0, heads, together):
+        own, carried = [], []
+        for place in range(together):
+            j = start + place
+            rows = [normed[j]] + [exchange(normed[j], "hidden", k, sides) for k in range(1, sides)]
+            part, *carried = ffn(rows, w_up, w_down, j, place, together, carried)
+            own.append(part)
         back = [
-            exchange(parts[k], "hidden", peer_step(k, sides), sides) for k in range(1, sides)
+            exchange(carried[k - 1], "hidden", peer_step(k, sides), sides) for k in range(1, sides)
         ]
-        terms.append([parts[0]] + back + [normed[j]])
-    return finish(terms, gain_out)
+        groups.append((own, normed[start : start + together], back))
+    return finish(groups, gain_out)
 
 
 def solution(mesh):

time: 51.3 us -> 50.1 us (0.977)
  starting transfers between devices: 21.2 us -> 19 us
  waiting for transfers between devices: 11.1 us -> 11.9 us
    ppermute x15 -> x13, starting transfers between devices: 21.2 us -> 19 us  [exchange(): lax.ppermute(value, axis, [(a, peer_of(a, step, count)) for a in range(co...]
    ppermute x15 -> x13, waiting for transfers between devices: 11.1 us -> 11.9 us  [exchange(): lax.ppermute(value, axis, [(a, peer_of(a, step, count)) for a in range(co...]
    pallas_call x5 -> x6, Pallas kernels: 8.33 us -> 8.49 us  [the longest x4 7.01 us: ffn(): pl.pallas_call(lambda *refs: ffn_kernel((j, peers, place), *refs), out_sh...]
  transfers between devices with their start and end apart: 15 -> 13, of which waited for: 4 -> 4; matrix products, arithmetic and copies ran while one was open for 0% -> 0% of each run, Pallas kernels for 16% -> 17%
where the time goes in v2:
time: 50.1 us; the launch traced here: 50 us
  starting transfers between devices  19 us (38%)
  Pallas kernels  18.7 us (37%)
  waiting for transfers between devices  11.9 us (24%)
    ppermute x13, starting transfers between devices, exchange(): lax.ppermute(value, axis, [(a, peer_of(a, step, count)) for a in range(co...  19 us
    ppermute x13, waiting for transfers between devices, exchange(): lax.ppermute(value, axis, [(a, peer_of(a, step, count)) for a in range(co...  11.9 us
    pallas_call x1, Pallas kernels, attention(): pl.pallas_call(lambda *refs: attention_kernel((tokens, heads, requests, h...  8.38 us
    pallas_call x4, Pallas kernels, ffn(): pl.pallas_call(lambda *refs: ffn_kernel((j, peers, place), *refs), out_sh...  7.01 us
    pallas_call x4, Pallas kernels, mix(): pl.pallas_call(lambda *refs: mix_kernel((tokens, heads, requests, width /...  1.72 us
    pallas_call x2, Pallas kernels, finish(): pl.pallas_call(lambda *refs, sizes=sizes, last=last: finish_kernel(sizes,...  1.48 us
  transfers between devices with their start and end apart: 13, of which 4 were waited for; matrix products, arithmetic and copies ran while one was open for 0% of the time, Pallas kernels for 17%

profile of v2, /device:TPU:0, one launch (start us, length us, event | category | flops | bytes accessed | tf_op | source)
XLA Modules:
  0.0 50.0 jit_solution(6545674349343146921)
XLA Ops:
  0.0 8.4 %attention.1.refs_0_ = f32[2,1088,128]{2,1,0:T(8,128)S(1)} custom-call(s32[128]{0:T(128)} %refs_0_.1, bf16[32,192]{1,0:T(8,128)(2,1)} %refs_1_.1, bf16[96,192,128]{2,1,0:T(8,128)(2,1)} %refs_2_.5, bf16[96,192,128]{2,1,0:T(8,128)(2,1)} %refs_3_.5), custom_call_target="tpu_custom_call" | custom-call | flops 1610612736 | bytes 9437184 | tf_op jit(solution)/shard_map/attention/pallas_call | solution.py:184
  8.4 0.0 copy-start
  8.4 0.0 slice-start.1
  8.5 0.0 slice-start.6
  8.5 0.1 pack.1
  8.6 3.0 %collective-permute-start = (bf16[128,192]{1,0:T(8,128)(2,1)S(1)}, bf16[128,192]{1,0:T(8,128)(2,1)S(1)}, u32[]{:S(2)}, u32[]{:S(2)}) collective-permute-start(bf16[128,192]{1,0:T(8,128)(2,1)S(1)} %get-tuple-element.24.refs_1_), channel_id=1, source_target_pairs={{0,2},{2,0},{4,6},{6,4},{8,10},{10,8},{12,14},{14,12},{1,3},{3,1},... | collective-permute-start | bytes 147464 | tf_op jit(solution)/shard_map/ppermute | solution.py:31
  11.6 1.6 %collective-permute-start.1 = (bf16[128,192]{1,0:T(8,128)(2,1)S(1)}, bf16[128,192]{1,0:T(8,128)(2,1)S(1)}, u32[]{:S(2)}, u32[]{:S(2)}) collective-permute-start(bf16[128,192]{1,0:T(8,128)(2,1)S(1)} %get-tuple-element.25.refs_2_), channel_id=1, source_target_pairs={{0,4},{2,6},{4,0},{6,2},{8,12},{10,14},{12,8},{14,10},{1,5},{3,7},... | collective-permute-start | bytes 147464 | tf_op jit(solution)/shard_map/ppermute | solution.py:31
  13.2 3.0 %collective-permute-start.3 = (bf16[128,192]{1,0:T(8,128)(2,1)S(1)}, bf16[128,192]{1,0:T(8,128)(2,1)S(1)}, u32[]{:S(2)}, u32[]{:S(2)}) collective-permute-start(bf16[128,192]{1,0:T(8,128)(2,1)S(1)} %get-tuple-element.27.refs_4_), channel_id=1, source_target_pairs={{0,8},{2,10},{4,12},{6,14},{8,0},{10,2},{12,4},{14,6},{1,9},{3,11}... | collective-permute-start | bytes 147464 | tf_op jit(solution)/shard_map/ppermute | solution.py:31
  16.2 1.3 %collective-permute-start.4 = (bf16[128,192]{1,0:T(8,128)(2,1)S(1)}, bf16[128,192]{1,0:T(8,128)(2,1)S(1)}, u32[]{:S(2)}, u32[]{:S(2)}) collective-permute-start(bf16[128,192]{1,0:T(8,128)(2,1)S(1)} %get-tuple-element.28.refs_5_), channel_id=1, source_target_pairs={{0,10},{2,8},{4,14},{6,12},{8,2},{10,0},{12,6},{14,4},{1,11},{3,9}... | collective-permute-start | bytes 147464 | tf_op jit(solution)/shard_map/ppermute | solution.py:31
  17.5 3.6 %collective-permute-start.5 = (bf16[128,192]{1,0:T(8,128)(2,1)S(1)}, bf16[128,192]{1,0:T(8,128)(2,1)S(1)}, u32[]{:S(2)}, u32[]{:S(2)}) collective-permute-start(bf16[128,192]{1,0:T(8,128)(2,1)S(1)} %get-tuple-element.29.refs_6_), channel_id=1, source_target_pairs={{0,12},{2,14},{4,8},{6,10},{8,4},{10,6},{12,0},{14,2},{1,13},{3,15... | collective-permute-start | bytes 147464 | tf_op jit(solution)/shard_map/ppermute | solution.py:31
  21.1 0.0 collective-permute-start.6
  21.1 5.2 %collective-permute-done.4.refs_13_ = bf16[128,192]{1,0:T(8,128)(2,1)S(1)} collective-permute-done((bf16[128,192]{1,0:T(8,128)(2,1)S(1)}, bf16[128,192]{1,0:T(8,128)(2,1)S(1)}, u32[]{:S(2)}, u32[]{:S(2)}) %collective-permute-start.4) | collective-permute-done | bytes 49184 | tf_op jit(solution)/shard_map/ppermute | solution.py:31
  26.4 1.7 %collective-permute-done.6.refs_15_ = bf16[128,192]{1,0:T(8,128)(2,1)S(1)} collective-permute-done((bf16[128,192]{1,0:T(8,128)(2,1)S(1)}, bf16[128,192]{1,0:T(8,128)(2,1)S(1)}, u32[]{:S(2)}, u32[]{:S(2)}) %collective-permute-start.6) | collective-permute-done | bytes 49184 | tf_op jit(solution)/shard_map/ppermute | solution.py:31
  28.1 0.4 mix.6.refs_0_.refs_2_
  28.6 1.6 %collective-permute-start.10 = (bf16[32,1536]{1,0:T(8,128)(2,1)S(1)}, bf16[32,1536]{1,0:T(8,128)(2,1)S(1)}, u32[]{:S(2)}, u32[]{:S(2)}) collective-permute-start(bf16[32,1536]{1,0:T(8,128)(2,1)S(1)} %mix.6.refs_0_.refs_2_), channel_id=1, source_target_pairs={{0,1},{1,0},{2,3},{3,2},{4,5},{5,4},{6,7},{7,6},{8,9},{9,8},{10,11... | collective-permute-start | bytes 294920 | tf_op jit(solution)/shard_map/ppermute | solution.py:31
  30.2 0.4 mix.7.refs_0_.refs_3_
  30.6 0.5 %collective-permute-start.11 = (bf16[32,1536]{1,0:T(8,128)(2,1)S(1)}, bf16[32,1536]{1,0:T(8,128)(2,1)S(1)}, u32[]{:S(2)}, u32[]{:S(2)}) collective-permute-start(bf16[32,1536]{1,0:T(8,128)(2,1)S(1)} %mix.7.refs_0_.refs_3_), channel_id=1, source_target_pairs={{0,1},{1,0},{2,3},{3,2},{4,5},{5,4},{6,7},{7,6},{8,9},{9,8},{10,11... | collective-permute-start | bytes 294920 | tf_op jit(solution)/shard_map/ppermute | solution.py:31
  31.1 0.5 mix.4.refs_0_.refs_2_
  31.6 1.6 %collective-permute-start.7 = (bf16[32,1536]{1,0:T(8,128)(2,1)S(1)}, bf16[32,1536]{1,0:T(8,128)(2,1)S(1)}, u32[]{:S(2)}, u32[]{:S(2)}) collective-permute-start(bf16[32,1536]{1,0:T(8,128)(2,1)S(1)} %mix.4.refs_0_.refs_2_), channel_id=1, source_target_pairs={{0,1},{1,0},{2,3},{3,2},{4,5},{5,4},{6,7},{7,6},{8,9},{9,8},{10,11... | collective-permute-start | bytes 294920 | tf_op jit(solution)/shard_map/ppermute | solution.py:31
  33.2 0.4 mix.5.refs_0_.refs_3_
  33.7 0.5 %collective-permute-start.8 = (bf16[32,1536]{1,0:T(8,128)(2,1)S(1)}, bf16[32,1536]{1,0:T(8,128)(2,1)S(1)}, u32[]{:S(2)}, u32[]{:S(2)}) collective-permute-start(bf16[32,1536]{1,0:T(8,128)(2,1)S(1)} %mix.5.refs_0_.refs_3_), channel_id=1, source_target_pairs={{0,1},{1,0},{2,3},{3,2},{4,5},{5,4},{6,7},{7,6},{8,9},{9,8},{10,11... | collective-permute-start | bytes 294920 | tf_op jit(solution)/shard_map/ppermute | solution.py:31
  34.3 1.8 %ffn.6 = (f32[32,1536]{1,0:T(8,128)S(1)}, bf16[64,1536]{1,0:T(8,128)(2,1)S(1)}) custom-call(bf16[32,1536]{1,0:T(8,128)(2,1)S(1)} %mix.6.refs_0_.refs_2_, bf16[32,1536]{1,0:T(8,128)(2,1)S(1)} %collective-permute-done.10.refs_1_, bf16[4,1536,1536]{2,1,0:T(8,128)(2,1)S(1)} %bitcast.1, bf16[4,1536,1536]{2,1,0:T(8,128)(2,1)S(1)} %bitcast.3), custom_call_target="tpu_custom_call" | custom-call | flops 603979776 | bytes 9437184 | tf_op jit(solution)/shard_map/ffn/pallas_call | solution.py:286
  36.1 1.8 %ffn.7 = (f32[32,1536]{1,0:T(8,128)S(1)}, bf16[64,1536]{1,0:T(8,128)(2,1)S(1)}) custom-call(bf16[32,1536]{1,0:T(8,128)(2,1)S(1)} %mix.7.refs_0_.refs_3_, bf16[32,1536]{1,0:T(8,128)(2,1)S(1)} %collective-permute-done.11.refs_1_, bf16[4,1536,1536]{2,1,0:T(8,128)(2,1)S(1)} %bitcast.1, ...), custom_call_target="tpu_custom_call", output_to_operand_aliasing={{1}: (4, {})} | custom-call | flops 603979776 | bytes 9437184 | tf_op jit(solution)/shard_map/ffn/pallas_call | solution.py:286
  37.8 1.6 %collective-permute-start.12 = (bf16[64,1536]{1,0:T(8,128)(2,1)S(1)}, bf16[64,1536]{1,0:T(8,128)(2,1)S(1)}, u32[]{:S(2)}, u32[]{:S(2)}) collective-permute-start(bf16[64,1536]{1,0:T(8,128)(2,1)S(1)} %get-tuple-element.38), channel_id=1, source_target_pairs={{0,1},{1,0},{2,3},{3,2},{4,5},{5,4},{6,7},{7,6},{8,9},{9,8},{10,11... | collective-permute-start | bytes 589832 | tf_op jit(solution)/shard_map/ppermute | solution.py:31
  39.5 1.8 %ffn.4 = (f32[32,1536]{1,0:T(8,128)S(1)}, bf16[64,1536]{1,0:T(8,128)(2,1)S(1)}) custom-call(bf16[32,1536]{1,0:T(8,128)(2,1)S(1)} %mix.4.refs_0_.refs_2_, bf16[32,1536]{1,0:T(8,128)(2,1)S(1)} %collective-permute-done.7.refs_1_, bf16[4,1536,1536]{2,1,0:T(8,128)(2,1)S(1)} %bitcast.1, bf16[4,1536,1536]{2,1,0:T(8,128)(2,1)S(1)} %bitcast.3), custom_call_target="tpu_custom_call" | custom-call | flops 603979776 | bytes 9437184 | tf_op jit(solution)/shard_map/ffn/pallas_call | solution.py:286
  41.2 0.0 copy-start.1
  41.2 1.8 %ffn.5 = (f32[32,1536]{1,0:T(8,128)S(1)}, bf16[64,1536]{1,0:T(8,128)(2,1)S(1)}) custom-call(bf16[32,1536]{1,0:T(8,128)(2,1)S(1)} %mix.5.refs_0_.refs_3_, bf16[32,1536]{1,0:T(8,128)(2,1)S(1)} %collective-permute-done.8.refs_1_, bf16[4,1536,1536]{2,1,0:T(8,128)(2,1)S(1)} %bitcast.1, ...), custom_call_target="tpu_custom_call", output_to_operand_aliasing={{1}: (4, {})} | custom-call | flops 603979776 | bytes 9437184 | tf_op jit(solution)/shard_map/ffn/pallas_call | solution.py:286
  43.0 0.5 %collective-permute-start.9 = (bf16[64,1536]{1,0:T(8,128)(2,1)S(1)}, bf16[64,1536]{1,0:T(8,128)(2,1)S(1)}, u32[]{:S(2)}, u32[]{:S(2)}) collective-permute-start(bf16[64,1536]{1,0:T(8,128)(2,1)S(1)} %get-tuple-element.34), channel_id=1, source_target_pairs={{0,1},{1,0},{2,3},{3,2},{4,5},{5,4},{6,7},{7,6},{8,9},{9,8},{10,11... | collective-permute-start | bytes 589832 | tf_op jit(solution)/shard_map/ppermute | solution.py:31
  43.6 1.9 %collective-permute-done.12.refs_4_ = bf16[64,1536]{1,0:T(8,128)(2,1)S(1)} collective-permute-done((bf16[64,1536]{1,0:T(8,128)(2,1)S(1)}, bf16[64,1536]{1,0:T(8,128)(2,1)S(1)}, u32[]{:S(2)}, u32[]{:S(2)}) %collective-permute-start.12) | collective-permute-done | bytes 196640 | tf_op jit(solution)/shard_map/ppermute | solution.py:31
  45.5 0.2 finish_early.1
  45.7 3.0 %collective-permute-done.9.refs_4_ = bf16[64,1536]{1,0:T(8,128)(2,1)S(1)} collective-permute-done((bf16[64,1536]{1,0:T(8,128)(2,1)S(1)}, bf16[64,1536]{1,0:T(8,128)(2,1)S(1)}, u32[]{:S(2)}, u32[]{:S(2)}) %collective-permute-start.9) | collective-permute-done | bytes 196640 | tf_op jit(solution)/shard_map/ppermute | solution.py:31
  48.7 1.2 %finish.1 = bf16[32,4,1536]{2,1,0:T(4,128)(2,1)} custom-call(f32[32,1536]{1,0:T(8,128)S(1)} %get-tuple-element.31.refs_0_, f32[32,1536]{1,0:T(8,128)S(1)} %get-tuple-element.33.refs_1_, bf16[32,1536]{1,0:T(8,128)(2,1)S(1)} %mix.4.refs_0_.refs_2_, bf16[32,1536]{1,0:T(8,128)(2,1)S(1)} %mix.5.refs_0_.refs_3_, ...), custom_call_target="tpu_custom_call" | custom-call | flops 983040 | bytes 786432 | tf_op jit(solution)/shard_map/finish/pallas_call | solution.py:342
  (34 shorter events, 0.1 us)
Async XLA Ops:
  0.0 34.2 %slice-start = ((s8[18874368]{0:T(1024)(128)(4,1)}), s8[4194304]{0:T(1024)(128)(4,1)S(1)}, s32[]{:S(2)}) async-start(s8[18874368]{0:T(1024)(128)(4,1)} %bitcast), calls=%async_computation | async-start | bytes 8388608
  0.0 34.2 %slice-start.5 = ((s8[18874368]{0:T(1024)(128)(4,1)}), s8[2097152]{0:T(1024)(128)(4,1)S(1)}, s32[]{:S(2)}) async-start(s8[18874368]{0:T(1024)(128)(4,1)} %bitcast.2), calls=%async_computation.5 | async-start | bytes 4194304
  8.4 12.7 %copy-start = (f32[1536]{0:T(1024)S(1)}, f32[1536]{0:T(1024)}, u32[]{:S(2)}) copy-start(f32[1536]{0:T(1024)} %param.12) | copy-start | bytes 18436
  8.4 25.8 %slice-start.1 = ((s8[18874368]{0:T(1024)(128)(4,1)}), s8[4194304]{0:T(1024)(128)(4,1)S(1)}, s32[]{:S(2)}) async-start(s8[18874368]{0:T(1024)(128)(4,1)} %bitcast), calls=%async_computation.1 | async-start | bytes 8388608
  8.4 25.8 %slice-start.2 = ((s8[18874368]{0:T(1024)(128)(4,1)}), s8[4194304]{0:T(1024)(128)(4,1)S(1)}, s32[]{:S(2)}) async-start(s8[18874368]{0:T(1024)(128)(4,1)} %bitcast), calls=%async_computation.2 | async-start | bytes 8388608
  8.4 25.8 %slice-start.3 = ((s8[18874368]{0:T(1024)(128)(4,1)}), s8[4194304]{0:T(1024)(128)(4,1)S(1)}, s32[]{:S(2)}) async-start(s8[18874368]{0:T(1024)(128)(4,1)} %bitcast), calls=%async_computation.3 | async-start | bytes 8388608
  8.4 25.8 %slice-start.4 = ((s8[18874368]{0:T(1024)(128)(4,1)}), s8[2097152]{0:T(1024)(128)(4,1)S(1)}, s32[]{:S(2)}) async-start(s8[18874368]{0:T(1024)(128)(4,1)} %bitcast), calls=%async_computation.4 | async-start | bytes 4194304
  8.5 25.8 %slice-start.6 = ((s8[18874368]{0:T(1024)(128)(4,1)}), s8[4194304]{0:T(1024)(128)(4,1)S(1)}, s32[]{:S(2)}) async-start(s8[18874368]{0:T(1024)(128)(4,1)} %bitcast.2), calls=%async_computation.6 | async-start | bytes 8388608
  8.5 25.8 %slice-start.7 = ((s8[18874368]{0:T(1024)(128)(4,1)}), s8[4194304]{0:T(1024)(128)(4,1)S(1)}, s32[]{:S(2)}) async-start(s8[18874368]{0:T(1024)(128)(4,1)} %bitcast.2), calls=%async_computation.7 | async-start | bytes 8388608
  8.5 25.8 %slice-start.8 = ((s8[18874368]{0:T(1024)(128)(4,1)}), s8[4194304]{0:T(1024)(128)(4,1)S(1)}, s32[]{:S(2)}) async-start(s8[18874368]{0:T(1024)(128)(4,1)} %bitcast.2), calls=%async_computation.8 | async-start | bytes 8388608
  8.5 25.8 %slice-start.9 = ((s8[18874368]{0:T(1024)(128)(4,1)}), s8[4194304]{0:T(1024)(128)(4,1)S(1)}, s32[]{:S(2)}) async-start(s8[18874368]{0:T(1024)(128)(4,1)} %bitcast.2), calls=%async_computation.9 | async-start | bytes 8388608
  8.6 8.9 %collective-permute-start = (bf16[128,192]{1,0:T(8,128)(2,1)S(1)}, bf16[128,192]{1,0:T(8,128)(2,1)S(1)}, u32[]{:S(2)}, u32[]{:S(2)}) collective-permute-start(bf16[128,192]{1,0:T(8,128)(2,1)S(1)} %get-tuple-element.24.refs_1_), channel_id=1, source_target_pairs={{0,2},{2,0},{4,6},{6,4},{8,10},{10,8},{12,14},{14,12},{1,3},{3,1},... | collective-permute-start | bytes 147464 | tf_op jit(solution)/shard_map/ppermute | solution.py:31
  11.6 9.5 %collective-permute-start.1 = (bf16[128,192]{1,0:T(8,128)(2,1)S(1)}, bf16[128,192]{1,0:T(8,128)(2,1)S(1)}, u32[]{:S(2)}, u32[]{:S(2)}) collective-permute-start(bf16[128,192]{1,0:T(8,128)(2,1)S(1)} %get-tuple-element.25.refs_2_), channel_id=1, source_target_pairs={{0,4},{2,6},{4,0},{6,2},{8,12},{10,14},{12,8},{14,10},{1,5},{3,7},... | collective-permute-start | bytes 147464 | tf_op jit(solution)/shard_map/ppermute | solution.py:31
  13.2 7.9 %collective-permute-start.2 = (bf16[128,192]{1,0:T(8,128)(2,1)S(1)}, bf16[128,192]{1,0:T(8,128)(2,1)S(1)}, u32[]{:S(2)}, u32[]{:S(2)}) collective-permute-start(bf16[128,192]{1,0:T(8,128)(2,1)S(1)} %get-tuple-element.26.refs_3_), channel_id=1, source_target_pairs={{0,6},{2,4},{4,2},{6,0},{8,14},{10,12},{12,10},{14,8},{1,7},{3,5},... | collective-permute-start | bytes 147464 | tf_op jit(solution)/shard_map/ppermute | solution.py:31
  13.2 7.9 %collective-permute-start.3 = (bf16[128,192]{1,0:T(8,128)(2,1)S(1)}, bf16[128,192]{1,0:T(8,128)(2,1)S(1)}, u32[]{:S(2)}, u32[]{:S(2)}) collective-permute-start(bf16[128,192]{1,0:T(8,128)(2,1)S(1)} %get-tuple-element.27.refs_4_), channel_id=1, source_target_pairs={{0,8},{2,10},{4,12},{6,14},{8,0},{10,2},{12,4},{14,6},{1,9},{3,11}... | collective-permute-start | bytes 147464 | tf_op jit(solution)/shard_map/ppermute | solution.py:31
  16.2 10.2 %collective-permute-start.4 = (bf16[128,192]{1,0:T(8,128)(2,1)S(1)}, bf16[128,192]{1,0:T(8,128)(2,1)S(1)}, u32[]{:S(2)}, u32[]{:S(2)}) collective-permute-start(bf16[128,192]{1,0:T(8,128)(2,1)S(1)} %get-tuple-element.28.refs_5_), channel_id=1, source_target_pairs={{0,10},{2,8},{4,14},{6,12},{8,2},{10,0},{12,6},{14,4},{1,11},{3,9}... | collective-permute-start | bytes 147464 | tf_op jit(solution)/shard_map/ppermute | solution.py:31
  17.5 8.9 %collective-permute-start.5 = (bf16[128,192]{1,0:T(8,128)(2,1)S(1)}, bf16[128,192]{1,0:T(8,128)(2,1)S(1)}, u32[]{:S(2)}, u32[]{:S(2)}) collective-permute-start(bf16[128,192]{1,0:T(8,128)(2,1)S(1)} %get-tuple-element.29.refs_6_), channel_id=1, source_target_pairs={{0,12},{2,14},{4,8},{6,10},{8,4},{10,6},{12,0},{14,2},{1,13},{3,15... | collective-permute-start | bytes 147464 | tf_op jit(solution)/shard_map/ppermute | solution.py:31
  21.1 7.1 %collective-permute-start.6 = (bf16[128,192]{1,0:T(8,128)(2,1)S(1)}, bf16[128,192]{1,0:T(8,128)(2,1)S(1)}, u32[]{:S(2)}, u32[]{:S(2)}) collective-permute-start(bf16[128,192]{1,0:T(8,128)(2,1)S(1)} %get-tuple-element.30.refs_7_), channel_id=1, source_target_pairs={{0,14},{2,12},{4,10},{6,8},{8,6},{10,4},{12,2},{14,0},{1,15},{3,13... | collective-permute-start | bytes 147464 | tf_op jit(solution)/shard_map/ppermute | solution.py:31
  28.6 5.6 %collective-permute-start.10 = (bf16[32,1536]{1,0:T(8,128)(2,1)S(1)}, bf16[32,1536]{1,0:T(8,128)(2,1)S(1)}, u32[]{:S(2)}, u32[]{:S(2)}) collective-permute-start(bf16[32,1536]{1,0:T(8,128)(2,1)S(1)} %mix.6.refs_0_.refs_2_), channel_id=1, source_target_pairs={{0,1},{1,0},{2,3},{3,2},{4,5},{5,4},{6,7},{7,6},{8,9},{9,8},{10,11... | collective-permute-start | bytes 294920 | tf_op jit(solution)/shard_map/ppermute | solution.py:31
  30.6 5.5 %collective-permute-start.11 = (bf16[32,1536]{1,0:T(8,128)(2,1)S(1)}, bf16[32,1536]{1,0:T(8,128)(2,1)S(1)}, u32[]{:S(2)}, u32[]{:S(2)}) collective-permute-start(bf16[32,1536]{1,0:T(8,128)(2,1)S(1)} %mix.7.refs_0_.refs_3_), channel_id=1, source_target_pairs={{0,1},{1,0},{2,3},{3,2},{4,5},{5,4},{6,7},{7,6},{8,9},{9,8},{10,11... | collective-permute-start | bytes 294920 | tf_op jit(solution)/shard_map/ppermute | solution.py:31
  31.6 7.8 %collective-permute-start.7 = (bf16[32,1536]{1,0:T(8,128)(2,1)S(1)}, bf16[32,1536]{1,0:T(8,128)(2,1)S(1)}, u32[]{:S(2)}, u32[]{:S(2)}) collective-permute-start(bf16[32,1536]{1,0:T(8,128)(2,1)S(1)} %mix.4.refs_0_.refs_2_), channel_id=1, source_target_pairs={{0,1},{1,0},{2,3},{3,2},{4,5},{5,4},{6,7},{7,6},{8,9},{9,8},{10,11... | collective-permute-start | bytes 294920 | tf_op jit(solution)/shard_map/ppermute | solution.py:31
  33.7 7.6 %collective-permute-start.8 = (bf16[32,1536]{1,0:T(8,128)(2,1)S(1)}, bf16[32,1536]{1,0:T(8,128)(2,1)S(1)}, u32[]{:S(2)}, u32[]{:S(2)}) collective-permute-start(bf16[32,1536]{1,0:T(8,128)(2,1)S(1)} %mix.5.refs_0_.refs_3_), channel_id=1, source_target_pairs={{0,1},{1,0},{2,3},{3,2},{4,5},{5,4},{6,7},{7,6},{8,9},{9,8},{10,11... | collective-permute-start | bytes 294920 | tf_op jit(solution)/shard_map/ppermute | solution.py:31
  37.8 7.6 %collective-permute-start.12 = (bf16[64,1536]{1,0:T(8,128)(2,1)S(1)}, bf16[64,1536]{1,0:T(8,128)(2,1)S(1)}, u32[]{:S(2)}, u32[]{:S(2)}) collective-permute-start(bf16[64,1536]{1,0:T(8,128)(2,1)S(1)} %get-tuple-element.38), channel_id=1, source_target_pairs={{0,1},{1,0},{2,3},{3,2},{4,5},{5,4},{6,7},{7,6},{8,9},{9,8},{10,11... | collective-permute-start | bytes 589832 | tf_op jit(solution)/shard_map/ppermute | solution.py:31
  41.2 2.3 %copy-start.1 = (f32[1536]{0:T(1024)S(1)}, f32[1536]{0:T(1024)}, u32[]{:S(2)}) copy-start(f32[1536]{0:T(1024)} %param.15) | copy-start | bytes 18436
  43.0 5.7 %collective-permute-start.9 = (bf16[64,1536]{1,0:T(8,128)(2,1)S(1)}, bf16[64,1536]{1,0:T(8,128)(2,1)S(1)}, u32[]{:S(2)}, u32[]{:S(2)}) collective-permute-start(bf16[64,1536]{1,0:T(8,128)(2,1)S(1)} %get-tuple-element.34), channel_id=1, source_target_pairs={{0,1},{1,0},{2,3},{3,2},{4,5},{5,4},{6,7},{7,6},{8,9},{9,8},{10,11... | collective-permute-start | bytes 589832 | tf_op jit(solution)/shard_map/ppermute | solution.py:31
